TPU v7x, 128 devices: a whole 4x4x4 slice. The times are simulated.
128 devices in a mesh: dp: 128 (over x, z, y, core).
Axes of the slice: x: 4, y: 4, z: 4, core: 2. Of those that a mesh axis runs over, the one named last changes fastest.
Arguments:
- token_ids: int32 [131072], P('dp'), may hold values from 0 to 31999, as said below
- tokens: bfloat16 [131072, 4096], P('dp'), may hold values from -64 to 64
- frozen_weight: bfloat16 [4096, 1024], replicated, may hold values from -0.09375 to 0.09375
- adapter_down: bfloat16 [4096, 128], replicated, may hold values from -0.09375 to 0.09375
- adapter_up: bfloat16 [128, 1024], replicated, may hold values from -1.5 to 1.5
- gate_weight: bfloat16 [4096, 8], replicated, may hold values from -1 to 1
- upstream: bfloat16 [131072, 1024], P('dp'), may hold values from -6 to 6
Outputs:
- projected: bfloat16 [131072, 1024], P('dp')
- input_grad: bfloat16 [131072, 4096], P('dp')
- clipped_down: float32 [4096, 128], replicated
- clipped_up: float32 [128, 1024], replicated
- clipped_gate: float32 [4096, 8], replicated
- load: float32 [8], replicated
- entropy: float32 [], replicated
Inputs may be any that keep to these rules, and one draw needn't show every extreme that they name: `token_ids`: within each device's block of 1024 tokens the live tokens (id not 0) come first, 256 or more of them, and padding (id 0) fills the rest; the last block is wholly live.
All inputs are finite; a program needn't handle non-finite values.
Results may differ from a plain program's by a relative error of at most 0.0095.
Values sent between devices are 32-bit elements; how exact they have to be, the bound alone decides.
A program may use at most 192 MiB of HBM per device.

v0:
```python
import math

import jax
import jax.numpy as jnp
from jax import lax
from jax.sharding import Mesh
from jax.sharding import PartitionSpec as P

DP = ("dp_0", "dp_1", "dp_2", "dp_3")


def over_axes(x, axes):
    for axis in axes:
        x = lax.psum(x, axis)
    return x


def left_dot(first, second):
    return lax.dot_general(
        first, second, (((0,), (0,)), ((), ())), preferred_element_type=jnp.float32
    )


def right_dot(first, second):
    return lax.dot_general(
        first, second, (((1,), (1,)), ((), ())), preferred_element_type=jnp.float32
    )


def exact_left(tokens, matrix):
    upper = matrix.astype(jnp.bfloat16)
    lower = (matrix - upper.astype(jnp.float32)).astype(jnp.bfloat16)
    return left_dot(tokens, upper) + left_dot(tokens, lower)


def share_stats(local):
    return (over_axes(local[0], DP), over_axes(local[1], DP), over_axes(local[2], DP))


def reduce_clip(terms, finish, limit):
    summed = lax.psum((terms[0], terms[1], terms[2]), DP)
    grads = finish(summed)
    total = (
        jnp.sum(grads[0] * grads[0]) + jnp.sum(grads[1] * grads[1]) + jnp.sum(grads[2] * grads[2])
    )
    factor = jnp.minimum(1.0, limit / jnp.sqrt(total))
    return (grads[0] * factor, grads[1] * factor, grads[2] * factor)


def on_device(token_ids, tokens, frozen_weight, adapter_down, adapter_up, gate_weight, upstream):
    width = tokens.shape[1]
    experts = gate_weight.shape[1]
    ranks = adapter_down.shape[1]
    rank = ranks // experts
    outputs = frozen_weight.shape[1]
    rows = tokens.shape[0]
    live = (token_ids != 0).astype(jnp.float32)
    base = jnp.dot(tokens, frozen_weight, preferred_element_type=jnp.float32)
    logits = jnp.dot(tokens, gate_weight, preferred_element_type=jnp.float32)
    prob = jax.nn.softmax(logits, axis=1)
    logp = jax.nn.log_softmax(logits, axis=1)
    low = jnp.dot(tokens, adapter_down, preferred_element_type=jnp.float32).astype(jnp.bfloat16)
    spread = jnp.repeat(prob, rank, axis=1)
    weighted = (low.astype(jnp.float32) * spread).astype(jnp.bfloat16)
    projected = (
        base + 2.0 * jnp.dot(weighted, adapter_up, preferred_element_type=jnp.float32)
    ).astype(jnp.bfloat16)
    masked = upstream * live.astype(jnp.bfloat16)[:, None]
    grad_up = 2.0 * left_dot(weighted, masked)
    back = right_dot(masked, adapter_up)
    gate_task = 2.0 * jnp.sum((low.astype(jnp.float32) * back).reshape(rows, experts, rank), axis=2)
    low_grad = (2.0 * spread * back).astype(jnp.bfloat16)
    grad_down = left_dot(tokens, low_grad)
    ent_tok = -jnp.sum(prob * logp, axis=1)
    local_stats = (jnp.sum(live[:, None] * prob, axis=0), jnp.sum(live * ent_tok), jnp.sum(live))

    def jac(vector):
        return prob * (vector - jnp.sum(prob * vector, axis=1, keepdims=True))

    plain_z = jac(gate_task) + 50.0 * live[:, None] * prob * (logp + ent_tok[:, None])
    frozen_back = right_dot(masked, frozen_weight) + right_dot(low_grad, adapter_down)
    count = width * ranks + ranks * outputs + width * experts
    limit = math.sqrt(count)
    load_all, ent_all, live_all = share_stats(local_stats)
    gate_z = plain_z + 2.0 * experts * 100.0 / live_all * live[:, None] * jac(load_all[None, :])
    terms = (grad_down, grad_up, exact_left(tokens, gate_z))

    def finish(summed):
        return summed

    clipped = reduce_clip(terms, finish, limit)
    input_grad = frozen_back + jnp.dot(
        gate_z, gate_weight.astype(jnp.float32).T, precision=lax.Precision.HIGHEST
    )
    return (
        projected,
        input_grad.astype(jnp.bfloat16),
        clipped[0],
        clipped[1],
        clipped[2],
        load_all / live_all,
        ent_all / live_all,
    )


def solution(mesh):
    torus = Mesh(mesh.devices.reshape(4, 4, 4, 2), ("dp_0", "dp_1", "dp_2", "dp_3"))
    return jax.shard_map(
        on_device,
        mesh=torus,
        in_specs=(P(DP), P(DP, None), P(), P(), P(), P(), P(DP, None)),
        out_specs=(P(DP, None), P(DP, None), P(), P(), P(), P(), P()),
        check_vma=False,
    )
```

profile of v0, /device:TPU:1, one launch (start us, length us, event | category | flops | bytes accessed | tf_op | source)
XLA Modules:
  0.0 243.0 jit_solution(7929073517609321213)
XLA Ops:
  7.2 0.0 copy-start
  7.2 0.0 all-reduce.7.cloned.1.call-start
  7.2 0.0 copy-start.1
  7.2 5.8 %fusion.21 = (f32[1024]{0:T(1024)S(1)}, f32[1024,8]{0,1:T(8,128)S(1)}) fusion(bf16[1024,4096]{1,0:T(8,128)(2,1)} %param.8, bf16[4096,8]{0,1:T(8,128)(2,1)} %param.12), kind=kOutput, calls=%fused_computation.48 | convolution fusion | flops 67116032 | bytes 8491008 | tf_op jit(solution)/shard_map/dot_general | solution.py:59
  13.1 0.0 copy-start.8
  13.1 0.0 copy-start.2
  13.1 0.0 copy-start.3
  13.2 0.0 copy-done
  13.2 0.1 copy-done.1
  13.3 2.9 %fusion.10 = f32[1024,128]{0,1:T(8,128)S(1)} fusion(bf16[1024,4096]{1,0:T(8,128)(2,1)S(1)} %copy-done.1, bf16[4096,128]{1,0:T(8,128)(2,1)S(1)} %copy-done), kind=kOutput, calls=%fused_computation.14 | convolution fusion | flops 1074003968 | bytes 9961472 | tf_op jit(solution)/shard_map/dot_general | solution.py:62
  16.2 0.0 copy-done.8
  16.2 0.0 copy-done.2
  16.3 0.0 copy-done.3
  16.3 1.5 fusion.16
  17.8 0.1 bitcast_reduce_fusion
  17.9 0.1 multiply_reduce_fusion.6
  18.0 0.6 select_reduce_fusion
  18.6 9.9 %all-reduce.3 = (f32[8]{0:T(128)S(1)}, f32[]{:T(128)}, f32[]{:T(128)}) all-reduce(f32[8]{0:T(128)S(1)} %get-tuple-element.16, f32[]{:T(128)} %get-tuple-element.18, f32[]{:T(128)} %get-tuple-element.17), channel_id=1, replica_groups=mesh['dp_0'=4,'dp_1'=4,'dp_2'=4,'dp_3'=2] {'dp_0'}, use_global_device_ids=true, to_apply=%region_11.12 | all-reduce | flops 10 | bytes 80 | tf_op jit(solution)/shard_map/psum | solution.py:14
  28.5 10.4 %all-reduce.2 = (f32[8]{0:T(128)S(1)}, f32[]{:T(128)}, f32[]{:T(128)}) all-reduce(f32[8]{0:T(128)S(1)} %get-tuple-element.28, f32[]{:T(128)} %get-tuple-element.29, f32[]{:T(128)} %get-tuple-element.30), channel_id=1, replica_groups=mesh['dp_0'=4,'dp_1'=4,'dp_2'=4,'dp_3'=2] {'dp_1'}, use_global_device_ids=true, to_apply=%region_12.13 | all-reduce | flops 10 | bytes 80 | tf_op jit(solution)/shard_map/psum | solution.py:14
  38.9 9.3 %all-reduce.1 = (f32[8]{0:T(128)S(1)}, f32[]{:T(128)}, f32[]{:T(128)}) all-reduce(f32[8]{0:T(128)S(1)} %get-tuple-element.25, f32[]{:T(128)} %get-tuple-element.26, f32[]{:T(128)} %get-tuple-element.27), channel_id=1, replica_groups=mesh['dp_0'=4,'dp_1'=4,'dp_2'=4,'dp_3'=2] {'dp_2'}, use_global_device_ids=true, to_apply=%region_13.14 | all-reduce | flops 10 | bytes 80 | tf_op jit(solution)/shard_map/psum | solution.py:14
  48.2 9.5 %all-reduce.4 = (f32[8]{0:T(128)S(1)}, f32[]{:T(128)}, f32[]{:T(128)}) all-reduce(f32[8]{0:T(128)S(1)} %get-tuple-element.22, f32[]{:T(128)} %get-tuple-element.23, f32[]{:T(128)} %get-tuple-element.24), channel_id=1, replica_groups=mesh['dp_0'=4,'dp_1'=4,'dp_2'=4,'dp_3'=2] {'dp_3'}, use_global_device_ids=true, to_apply=%region_14.15 | all-reduce | flops 10 | bytes 80 | tf_op jit(solution)/shard_map/psum | solution.py:14
  57.7 0.1 multiply_reduce_fusion.3
  58.4 0.0 copy-start.5
  58.5 6.0 %convolution_bitcast_fusion = f32[4096,128]{0,1:T(8,128)} fusion(bf16[1024,128]{0,1:T(8,128)(2,1)S(1)} %get-tuple-element.36, bf16[1024,4096]{1,0:T(8,128)(2,1)} %param.8), kind=kOutput, calls=%fused_computation.1 | convolution fusion | flops 1073741824 | bytes 10747904 | tf_op jit(solution)/shard_map/dot_general | solution.py:19
  64.5 0.0 copy-done.5
  64.5 0.0 slice-start
  64.5 1.3 fusion.7
  65.8 0.1 multiply_add_fusion
  65.9 0.0 slice-start.1
  65.9 4.7 %fusion.18 = f32[8,4096]{1,0:T(8,128)S(1)} fusion(bf16[1024,4096]{1,0:T(8,128)(2,1)} %param.8, f32[1024,8]{0,1:T(8,128)S(1)} %multiply_add_fusion), kind=kOutput, calls=%fused_computation.38 | convolution fusion | flops 67117056 | bytes 8552448 | tf_op jit(solution)/shard_map/dot_general | solution.py:19
  70.6 0.0 slice-done
  70.6 0.1 slice-done.1
  70.7 0.0 copy-start.7
  70.7 1.9 fusion
  72.6 0.0 all-reduce.7.cloned.1.call-update
  72.6 0.0 copy-done.7
  72.6 10.4 %fusion.23 = f32[1024,4096]{1,0:T(8,128)} fusion(f32[1024,8]{0,1:T(8,128)S(1)} %multiply_add_fusion, bf16[4096,8]{0,1:T(8,128)(2,1)S(1)} %copy-done.7), kind=kOutput, calls=%fused_computation.50 | convolution fusion | flops 402653184 | bytes 16875520 | tf_op jit(solution)/shard_map/dot_general | solution.py:92
  83.0 12.7 %fusion.22 = f32[1024,1024]{1,0:T(8,128)S(1)} fusion(bf16[1024,4096]{1,0:T(8,128)(2,1)} %param.8, bf16[4096,1024]{1,0:T(8,128)(2,1)} %param.9), kind=kOutput, calls=%fused_computation.49 | convolution fusion | flops 8589934592 | bytes 20971520 | tf_op jit(solution)/shard_map/dot_general | solution.py:58
  95.7 0.0 copy-start.4
  95.7 0.0 copy-start.6
  95.8 14.6 %fusion.5 = f32[1024,4096]{1,0:T(8,128)} fusion(bf16[4096,1024]{1,0:T(8,128)(2,1)} %param.9, bf16[1024,1024]{1,0:T(8,128)(2,1)S(1)} %copy-done.2, bf16[1024]{0:T(1024)(128)(2,1)S(1)} %get-tuple-element.41), kind=kOutput, calls=%fused_computation.10 | convolution fusion | flops 8590983168 | bytes 27265024 | tf_op jit(solution)/shard_map/dot_general | solution.py:25
  110.3 1.2 broadcast_divide_fusion
  111.5 0.0 copy-done.4
  111.5 0.0 copy-done.6
  111.5 2.1 add_convert_fusion.1
  114.9 15.4 %add_convert_fusion = bf16[1024,4096]{1,0:T(8,128)(2,1)} fusion(f32[1024,4096]{1,0:T(8,128)} %fusion.23, f32[1024,4096]{1,0:T(8,128)} %fusion.5, bf16[1024,128]{0,1:T(8,128)(2,1)S(1)} %get-tuple-element.36, bf16[4096,128]{1,0:T(8,128)(2,1)S(1)} %copy-done), kind=kOutput, calls=%fused_computation | convolution fusion | flops 1086324736 | bytes 43253760 | tf_op jit(solution)/shard_map/dot_general | solution.py:25
  130.3 89.6 %all-reduce.7.cloned.1.call-done = (f32[4096,128]{0,1:T(8,128)}, f32[128,1024]{1,0:T(8,128)}, f32[4096,8]{0,1:T(8,128)}) async-done(((f32[4096,128]{0,1:T(8,128)}, f32[128,1024]{1,0:T(8,128)}, f32[4096,8]{0,1:T(8,128)}), (f32[4096,128]{0,1:T(8,128)}, f32[128,1024]{1,0:T(8,128)}, f32[4096,8]{0,1:T(8,128)})) %all-reduce.7.cloned.1.call-update) | async-done | bytes 2752528 | tf_op jit(solution)/shard_map/psum | solution.py:41
  219.9 2.7 %multiply_reduce_fusion = f32[]{:T(128)} fusion(f32[4096,128]{0,1:T(8,128)} %get-tuple-element.19), kind=kLoop, calls=%fused_computation.5 | loop fusion | flops 1048575 | bytes 2097156 | tf_op jit(solution)/shard_map/reduce_sum | solution.py:44
  222.6 1.8 multiply_reduce_fusion.1
  224.4 1.5 multiply_reduce_fusion.2
  227.9 1.8 broadcast_multiply_fusion
  229.7 1.9 broadcast_multiply_fusion.1
  231.6 1.6 broadcast_multiply_fusion.2
  233.2 1.8 copy.14
  (7 shorter events, 0.1 us)
Async XLA Ops:
  7.2 6.0 %copy-start = (bf16[4096,128]{1,0:T(8,128)(2,1)S(1)}, bf16[4096,128]{1,0:T(8,128)(2,1)}, u32[]{:S(2)}) copy-start(bf16[4096,128]{1,0:T(8,128)(2,1)} %param.10) | copy-start | bytes 3145732
  7.2 212.7 %all-reduce.7.cloned.1.call-start = ((), (), s32[]{:S(2)}) async-start(), calls=%async_computation | async-start | bytes 5505024 | tf_op jit(solution)/shard_map/psum | solution.py:41
  7.2 6.1 %copy-start.1 = (bf16[1024,4096]{1,0:T(8,128)(2,1)S(1)}, bf16[1024,4096]{1,0:T(8,128)(2,1)}, u32[]{:S(2)}) copy-start(bf16[1024,4096]{1,0:T(8,128)(2,1)} %param.8) | copy-start | bytes 25165828
  13.1 3.2 %copy-start.8 = (s32[1024]{0:T(1024)S(1)}, s32[1024]{0:T(1024)}, u32[]{:S(2)}) copy-start(s32[1024]{0:T(1024)} %param.7) | copy-start | bytes 12292
  13.1 3.2 %copy-start.2 = (bf16[1024,1024]{1,0:T(8,128)(2,1)S(1)}, bf16[1024,1024]{1,0:T(8,128)(2,1)}, u32[]{:S(2)}) copy-start(bf16[1024,1024]{1,0:T(8,128)(2,1)} %param.13) | copy-start | bytes 6291460
  13.1 3.2 %copy-start.3 = (bf16[128,1024]{1,0:T(8,128)(2,1)S(1)}, bf16[128,1024]{1,0:T(8,128)(2,1)}, u32[]{:S(2)}) copy-start(bf16[128,1024]{1,0:T(8,128)(2,1)} %param.11) | copy-start | bytes 786436
  58.4 6.0 %copy-start.5 = (bf16[1024,128]{0,1:T(8,128)(2,1)S(1)}, bf16[1024,128]{0,1:T(8,128)(2,1)}, u32[]{:S(2)}) copy-start(bf16[1024,128]{0,1:T(8,128)(2,1)} %get-tuple-element.38) | copy-start | bytes 786436
  64.5 6.1 %slice-start = ((s8[8388608]{0:T(1024)(128)(4,1)}), s8[4194304]{0:T(1024)(128)(4,1)S(1)}, s32[]{:S(2)}) async-start(s8[8388608]{0:T(1024)(128)(4,1)} %bitcast.34), calls=%async_computation.1 | async-start | bytes 8388608
  65.9 4.9 %slice-start.1 = ((s8[8388608]{0:T(1024)(128)(4,1)}), s8[4194304]{0:T(1024)(128)(4,1)S(1)}, s32[]{:S(2)}) async-start(s8[8388608]{0:T(1024)(128)(4,1)} %bitcast.34), calls=%async_computation.2 | async-start | bytes 8388608
  70.7 1.9 copy-start.7
  95.7 15.8 %copy-start.4 = (bf16[128,1024]{1,0:T(8,128)(2,1)S(1)}, bf16[128,1024]{1,0:T(8,128)(2,1)}, u32[]{:S(2)}) copy-start(bf16[128,1024]{1,0:T(8,128)(2,1)} %param.11) | copy-start | bytes 786436
  95.7 15.7 %copy-start.6 = (bf16[1024,128]{0,1:T(8,128)(2,1)S(1)}, bf16[1024,128]{0,1:T(8,128)(2,1)}, u32[]{:S(2)}) copy-start(bf16[1024,128]{0,1:T(8,128)(2,1)} %get-tuple-element.38) | copy-start | bytes 786436
Sparse Core Ops, SparseCore 0:
  72.7 147.1 all-reduce.6
where the time goes:
time: 243 us
  waiting for transfers between devices  89.6 us (37%)
  matrix products  79.3 us (33%)
  blocking collectives  39.1 us (16%)
  between operations  19.4 us (8%)
  other arithmetic  13.5 us (6%)
    psum x1, waiting for transfers between devices, reduce_clip(): summed = lax.psum((terms[0], terms[1], terms[2]), DP)  89.6 us
    psum x4, blocking collectives, over_axes(): x = lax.psum(x, axis)  39.1 us
    dot_general x3, matrix products, right_dot(): lax.dot_general(first, second, (((1,), (1,)), ((), ())), preferred_elemen...  31.5 us
    dot_general x4, matrix products, left_dot(): lax.dot_general(first, second, (((0,), (0,)), ((), ())), preferred_elemen...  13.9 us
    dot_general x1, matrix products, on_device(): base = jnp.dot(tokens, frozen_weight, preferred_element_type=jnp.float32)  12.7 us
    dot_general x1, matrix products, on_device(): jnp.dot(gate_z, gate_weight.astype(jnp.float32).T, precision=lax.Precisio...  10.4 us
    dot_general x1, matrix products, on_device(): logits = jnp.dot(tokens, gate_weight, preferred_element_type=jnp.float32)  5.81 us
    mul x3, other arithmetic, reduce_clip(): return (grads[0] * factor, grads[1] * factor, grads[2] * factor)  5.23 us
  transfers between devices with their start and end apart: 1, of which 1 were waited for; matrix products, arithmetic and copies ran while one was open for 23% of the time, Pallas kernels for 0%

commit v1 on v0

--- a/solution.py
+++ b/solution.py
@@ -1,18 +1,21 @@
+import functools
 import math
 
 import jax
 import jax.numpy as jnp
 from jax import lax
+from jax.experimental import pallas as pl
+from jax.experimental.pallas import tpu as pltpu
 from jax.sharding import Mesh
 from jax.sharding import PartitionSpec as P
 
-DP = ("dp_0", "dp_1", "dp_2", "dp_3")
-
-
-def over_axes(x, axes):
-    for axis in axes:
-        x = lax.psum(x, axis)
-    return x
+AXES = ("dp_0", "dp_1", "dp_2")
+CORE = "dp_3"
+DP = AXES + (CORE,)
+MESH = pl.DeviceIdType.MESH
+SIDE = 4
+COLOURS = 3
+LANES = 128
 
 
 def left_dot(first, second):
@@ -33,18 +36,178 @@
     return left_dot(tokens, upper) + left_dot(tokens, lower)
 
 
-def share_stats(local):
-    return (over_axes(local[0], DP), over_axes(local[1], DP), over_axes(local[2], DP))
-
-
-def reduce_clip(terms, finish, limit):
-    summed = lax.psum((terms[0], terms[1], terms[2]), DP)
-    grads = finish(summed)
-    total = (
-        jnp.sum(grads[0] * grads[0]) + jnp.sum(grads[1] * grads[1]) + jnp.sum(grads[2] * grads[2])
-    )
-    factor = jnp.minimum(1.0, limit / jnp.sqrt(total))
-    return (grads[0] * factor, grads[1] * factor, grads[2] * factor)
+def ring_peer(axis, distance):
+    return {axis: lax.rem(lax.axis_index(axis) + distance, SIDE)}
+
+
+class Exchange:
+    def __init__(self, rows, part, total, halves, firsts, seconds, thirds, send, recv):
+        self.part, self.total = part, total
+        self.halves, self.firsts, self.seconds, self.thirds = halves, firsts, seconds, thirds
+        self.send, self.recv = send, recv
+        self.colour_rows = rows // COLOURS
+        self.half = self.colour_rows // 2
+        self.quarter = self.half // SIDE
+        self.last = self.quarter // SIDE
+        self.core = lax.axis_index(CORE)
+
+    def order(self, colour):
+        return tuple(AXES[(colour + step) % 3] for step in range(3))
+
+    def half_at(self, colour, core):
+        return colour * self.colour_rows + core * self.half
+
+    def quarter_at(self, colour, place):
+        return self.half_at(colour, self.core) + place * self.quarter
+
+    def last_at(self, colour, place, second):
+        return self.quarter_at(colour, place) + second * self.last
+
+    def copy(self, source, target, phase, colour, slot, device):
+        return pltpu.make_async_remote_copy(
+            src_ref=source,
+            dst_ref=target,
+            send_sem=self.send.at[phase, colour, slot],
+            recv_sem=self.recv.at[phase, colour, slot],
+            device_id=device,
+            device_id_type=MESH,
+        )
+
+    def rows_of(self, ref, start, size):
+        return ref.at[pl.ds(pl.multiple_of(start, 8), size)]
+
+    def copies(self, phase, colour):
+        first, second, third = self.order(colour)
+        one, two = lax.axis_index(first), lax.axis_index(second)
+        made = []
+        if phase == 0:
+            source = self.rows_of(self.part, self.half_at(colour, 1 - self.core), self.half)
+            made.append(self.copy(source, self.halves.at[colour], 0, colour, 0, {CORE: 1 - self.core}))
+        elif phase == 6:
+            here = self.half_at(colour, self.core)
+            made.append(
+                self.copy(
+                    self.rows_of(self.total, here, self.half),
+                    self.rows_of(self.total, here, self.half),
+                    6, colour, 0, {CORE: 1 - self.core},
+                )
+            )
+        else:
+            for distance in (1, 2, 3):
+                slot = distance - 1
+                if phase == 1:
+                    place = lax.rem(one + distance, SIDE)
+                    source = self.rows_of(self.part, self.quarter_at(colour, place), self.quarter)
+                    target, axis = self.firsts.at[colour, slot], first
+                elif phase == 2:
+                    place = lax.rem(two + distance, SIDE)
+                    source = self.rows_of(self.part, self.last_at(colour, one, place), self.last)
+                    target, axis = self.seconds.at[colour, slot], second
+                elif phase == 3:
+                    source = self.rows_of(self.part, self.last_at(colour, one, two), self.last)
+                    target, axis = self.thirds.at[colour, lax.axis_index(third)], third
+                elif phase == 4:
+                    source = self.rows_of(self.total, self.last_at(colour, one, two), self.last)
+                    target, axis = source, second
+                else:
+                    source = self.rows_of(self.total, self.quarter_at(colour, one), self.quarter)
+                    target, axis = source, first
+                made.append(self.copy(source, target, phase, colour, slot, ring_peer(axis, distance)))
+        return made
+
+    def start(self, phase, colour):
+        for copy in self.copies(phase, colour):
+            copy.start()
+
+    def finish(self, phase, colour):
+        for copy in self.copies(phase, colour):
+            copy.wait()
+        first, second, third = self.order(colour)
+        one, two = lax.axis_index(first), lax.axis_index(second)
+        if phase == 0:
+            here = pl.ds(pl.multiple_of(self.half_at(colour, self.core), 8), self.half)
+            self.part[here] = self.part[here] + self.halves[colour]
+        elif phase == 1:
+            here = pl.ds(pl.multiple_of(self.quarter_at(colour, one), 8), self.quarter)
+            got = self.firsts
+            self.part[here] = self.part[here] + got[colour, 0] + got[colour, 1] + got[colour, 2]
+        elif phase == 2:
+            here = pl.ds(pl.multiple_of(self.last_at(colour, one, two), 8), self.last)
+            got = self.seconds
+            mine = self.part[here] + got[colour, 0] + got[colour, 1] + got[colour, 2]
+            self.part[here] = mine
+        elif phase == 3:
+            here = pl.ds(pl.multiple_of(self.last_at(colour, one, two), 8), self.last)
+            got = self.thirds
+            got[colour, lax.axis_index(third)] = self.part[here]
+            self.total[here] = (got[colour, 0] + got[colour, 1]) + (got[colour, 2] + got[colour, 3])
+
+    def greet(self):
+        barrier = pltpu.get_barrier_semaphore()
+        peers = [{CORE: 1 - self.core}]
+        peers += [ring_peer(axis, distance) for axis in AXES for distance in (1, 2, 3)]
+        for peer in peers:
+            pl.semaphore_signal(barrier, inc=1, device_id=peer, device_id_type=MESH)
+        pl.semaphore_wait(barrier, len(peers))
+
+
+def reduce_kernel(limit, down_rows, up_blocks, gate_rows, part_ref, down_ref, up_ref, gate_ref, part, total, halves, firsts, seconds, thirds, send, recv):
+    rows = part.shape[0]
+    part[...] = part_ref[...]
+    exchange = Exchange(rows, part, total, halves, firsts, seconds, thirds, send, recv)
+    exchange.greet()
+    for colour in range(COLOURS):
+        exchange.start(0, colour)
+    for phase in range(7):
+        for colour in range(COLOURS):
+            exchange.finish(phase, colour)
+            if phase < 6:
+                exchange.start(phase + 1, colour)
+    values = total[...]
+    norm = jnp.sum(values * values)
+    factor = jnp.minimum(1.0, limit / jnp.sqrt(jnp.full((8, LANES), norm, jnp.float32)))[0:1]
+    down_ref[...] = total[0:down_rows] * factor
+    for block in range(up_blocks):
+        here = down_rows + block * LANES
+        up_ref[:, block * LANES : (block + 1) * LANES] = total[here : here + LANES] * factor
+    base = down_rows + up_blocks * LANES
+    for block in range(gate_rows // 8):
+        here = base + block * 8
+        gate_ref[:, block * LANES : (block + 1) * LANES] = total[here : here + 8] * factor
+
+
+def reduce_clip(down, up, gate, limit):
+    experts = gate.shape[1]
+    wide = lambda m: m.reshape(m.shape[0], -1, LANES).transpose(1, 0, 2).reshape(-1, LANES)
+    part = jnp.concatenate([down, wide(up), wide(gate.T)], axis=0)
+    rows = part.shape[0]
+    half = rows // COLOURS // 2
+    vmem = pl.BlockSpec(memory_space=pltpu.VMEM)
+    clipped = pl.pallas_call(
+        functools.partial(
+            reduce_kernel, limit, down.shape[0], up.shape[1] // LANES, gate.shape[0] * experts // LANES
+        ),
+        out_shape=(
+            jax.ShapeDtypeStruct(down.shape, jnp.float32),
+            jax.ShapeDtypeStruct(up.shape, jnp.float32),
+            jax.ShapeDtypeStruct((experts, gate.shape[0]), jnp.float32),
+        ),
+        in_specs=[vmem],
+        out_specs=(vmem, vmem, vmem),
+        scratch_shapes=[
+            pltpu.VMEM((rows, LANES), jnp.float32),
+            pltpu.VMEM((rows, LANES), jnp.float32),
+            pltpu.VMEM((COLOURS, half, LANES), jnp.float32),
+            pltpu.VMEM((COLOURS, 3, half // 4, LANES), jnp.float32),
+            pltpu.VMEM((COLOURS, 3, half // 16, LANES), jnp.float32),
+            pltpu.VMEM((COLOURS, 4, half // 16, LANES), jnp.float32),
+            pltpu.SemaphoreType.DMA((7, COLOURS, 3)),
+            pltpu.SemaphoreType.DMA((7, COLOURS, 3)),
+        ],
+        compiler_params=pltpu.CompilerParams(collective_id=0, has_side_effects=True),
+        name="reduce_clip",
+    )(part)
+    return clipped[0], clipped[1], clipped[2].T
 
 
 def on_device(token_ids, tokens, frozen_weight, adapter_down, adapter_up, gate_weight, upstream):
@@ -72,7 +235,9 @@
     low_grad = (2.0 * spread * back).astype(jnp.bfloat16)
     grad_down = left_dot(tokens, low_grad)
     ent_tok = -jnp.sum(prob * logp, axis=1)
-    local_stats = (jnp.sum(live[:, None] * prob, axis=0), jnp.sum(live * ent_tok), jnp.sum(live))
+    local_stats = jnp.concatenate(
+        [jnp.sum(live[:, None] * prob, axis=0), jnp.stack([jnp.sum(live * ent_tok), jnp.sum(live)])]
+    )
 
     def jac(vector):
         return prob * (vector - jnp.sum(prob * vector, axis=1, keepdims=True))
@@ -81,14 +246,10 @@
     frozen_back = right_dot(masked, frozen_weight) + right_dot(low_grad, adapter_down)
     count = width * ranks + ranks * outputs + width * experts
     limit = math.sqrt(count)
-    load_all, ent_all, live_all = share_stats(local_stats)
+    stats = lax.psum(local_stats, DP)
+    load_all, ent_all, live_all = stats[:experts], stats[experts], stats[experts + 1]
     gate_z = plain_z + 2.0 * experts * 100.0 / live_all * live[:, None] * jac(load_all[None, :])
-    terms = (grad_down, grad_up, exact_left(tokens, gate_z))
-
-    def finish(summed):
-        return summed
-
-    clipped = reduce_clip(terms, finish, limit)
+    clipped = reduce_clip(grad_down, grad_up, exact_left(tokens, gate_z), limit)
     input_grad = frozen_back + jnp.dot(
         gate_z, gate_weight.astype(jnp.float32).T, precision=lax.Precision.HIGHEST
     )
@@ -104,7 +265,7 @@
 
 
 def solution(mesh):
-    torus = Mesh(mesh.devices.reshape(4, 4, 4, 2), ("dp_0", "dp_1", "dp_2", "dp_3"))
+    torus = Mesh(mesh.devices.reshape(4, 4, 4, 2), DP)
     return jax.shard_map(
         on_device,
         mesh=torus,

time: 243 us -> 200 us (0.82)
  waiting for transfers between devices: 89.6 us -> 0 us
  Pallas kernels: 0 us -> 39 us
  blocking collectives: 39.1 us -> 68.8 us
  between operations: 19.4 us -> 4.05 us
  other arithmetic: 13.5 us -> 5.31 us
    psum x1 -> x0, waiting for transfers between devices: 89.6 us -> none  [reduce_clip(): summed = lax.psum((terms[0], terms[1], terms[2]), DP)]
    pallas_call x0 -> x1, Pallas kernels: none -> 39 us  [reduce_clip(): pl.pallas_call(functools.partial(reduce_kernel, limit, down.shape[0], up....]
    psum x4 -> x1, blocking collectives: 39.1 us -> 68.8 us  [on_device(): stats = lax.psum(local_stats, DP)]
    reduce_sum x3 -> x0, other arithmetic: 6.05 us -> none  [the longest x1 2.73 us: reduce_clip(): jnp.sum(grads[0] * grads[0]) + jnp.sum(grads[1] * grads[1])]
    mul x3 -> x0, other arithmetic: 5.23 us -> none  [reduce_clip(): return (grads[0] * factor, grads[1] * factor, grads[2] * factor)]
    concatenate x0 -> x2, other arithmetic: none -> 3.1 us  [the longest x1 1.74 us: reduce_clip(): part = jnp.concatenate([down, wide(up), wide(gate.T)], axis=0)]
  transfers between devices with their start and end apart: 1 -> 0, of which waited for: 1 -> 0; matrix products, arithmetic and copies ran while one was open for 23% -> 0% of each run, Pallas kernels for 0% -> 0%
where the time goes in v1:
time: 200 us
  matrix products  79.3 us (40%)
  blocking collectives  68.8 us (34%)
  Pallas kernels  39 us (20%)
  other arithmetic  5.31 us (3%)
  between operations  4.05 us (2%)
  local copies, waits for them, and re-layouts  3.63 us (2%)
    psum x1, blocking collectives, on_device(): stats = lax.psum(local_stats, DP)  68.8 us
    pallas_call x1, Pallas kernels, reduce_clip(): pl.pallas_call(functools.partial(reduce_kernel, limit, down.shape[0], up....  39 us
    dot_general x3, matrix products, right_dot(): lax.dot_general(first, second, (((1,), (1,)), ((), ())), preferred_elemen...  31.4 us
    dot_general x4, matrix products, left_dot(): lax.dot_general(first, second, (((0,), (0,)), ((), ())), preferred_elemen...  13.5 us
    dot_general x1, matrix products, on_device(): base = jnp.dot(tokens, frozen_weight, preferred_element_type=jnp.float32)  12.7 us
    dot_general x1, matrix products, on_device(): jnp.dot(gate_z, gate_weight.astype(jnp.float32).T, precision=lax.Precisio...  11 us
    dot_general x1, matrix products, on_device(): logits = jnp.dot(tokens, gate_weight, preferred_element_type=jnp.float32)  5.82 us

profile of v1, /device:TPU:1, one launch (start us, length us, event | category | flops | bytes accessed | tf_op | source)
XLA Modules:
  0.0 200.1 jit_solution(9980872190373606843)
XLA Ops:
  0.6 0.0 copy-start
  0.6 0.0 copy-start.2
  0.7 0.0 copy-start.11
  0.7 5.8 %fusion.25 = (f32[1024]{0:T(1024)S(1)}, f32[1024,8]{0,1:T(8,128)S(1)}) fusion(bf16[1024,4096]{1,0:T(8,128)(2,1)} %param.8, bf16[4096,8]{0,1:T(8,128)(2,1)} %param.12), kind=kOutput, calls=%fused_computation.47 | convolution fusion | flops 67116032 | bytes 8491008 | tf_op jit(solution)/shard_map/dot_general | solution.py:222
  6.5 0.0 copy-start.3
  6.5 0.0 copy-start.5
  6.6 0.0 copy-done.11
  6.6 0.0 copy-done
  6.6 0.2 copy-done.2
  6.8 2.9 %fusion.12 = f32[1024,128]{0,1:T(8,128)S(1)} fusion(bf16[1024,4096]{1,0:T(8,128)(2,1)S(1)} %copy-done.2, bf16[4096,128]{1,0:T(8,128)(2,1)S(1)} %copy-done), kind=kOutput, calls=%fused_computation.14 | convolution fusion | flops 1074003968 | bytes 9961472 | tf_op jit(solution)/shard_map/dot_general | solution.py:225
  9.7 0.0 copy-done.3
  9.7 0.0 copy-done.5
  9.7 1.5 fusion.19
  11.2 0.1 bitcast_reduce_fusion
  11.3 0.1 multiply_reduce_fusion.3
  11.4 0.6 select_reduce_fusion
  12.0 1.4 pad_maximum_fusion.1
  13.4 68.8 %psum.7 = f32[10]{0:T(128)S(1)} all-reduce(f32[10]{0:T(128)S(1)} %pad_maximum_fusion.1), channel_id=1, replica_groups=mesh['dp_0'=4,'dp_1'=4,'dp_2'=4,'dp_3'=2] {'dp_0','dp_1','dp_2','dp_3'}, use_global_device_ids=true, to_apply=%region_8.9 | all-reduce | flops 10 | bytes 80 | tf_op jit(solution)/shard_map/psum | solution.py:249
  82.2 0.6 fusion.24
  82.8 1.2 broadcast_divide_fusion
  84.0 0.1 multiply_reduce_fusion
  84.8 0.1 multiply_add_fusion
  84.8 11.0 %fusion.27 = f32[1024,4096]{1,0:T(8,128)} fusion(f32[1024,8]{0,1:T(8,128)S(1)} %multiply_add_fusion, bf16[4096,8]{0,1:T(8,128)(2,1)} %param.12), kind=kOutput, calls=%fused_computation.49 | convolution fusion | flops 402653184 | bytes 16875520 | tf_op jit(solution)/shard_map/dot_general | solution.py:253
  95.8 14.5 %fusion.4 = f32[1024,4096]{1,0:T(8,128)} fusion(bf16[4096,1024]{1,0:T(8,128)(2,1)} %param.9, bf16[1024,1024]{1,0:T(8,128)(2,1)S(1)} %copy-done.3, bf16[1024]{0:T(1024)(128)(2,1)S(1)} %get-tuple-element.25), kind=kOutput, calls=%fused_computation.9 | convolution fusion | flops 8590983168 | bytes 27265024 | tf_op jit(solution)/shard_map/dot_general | solution.py:28
  110.3 15.4 %add_convert_fusion = bf16[1024,4096]{1,0:T(8,128)(2,1)} fusion(f32[1024,4096]{1,0:T(8,128)} %fusion.27, f32[1024,4096]{1,0:T(8,128)} %fusion.4, bf16[1024,128]{0,1:T(8,128)(2,1)S(1)} %get-tuple-element.20, bf16[4096,128]{1,0:T(8,128)(2,1)S(1)} %copy-done), kind=kOutput, calls=%fused_computation | convolution fusion | flops 1086324736 | bytes 43253760 | tf_op jit(solution)/shard_map/dot_general | solution.py:28
  125.7 0.0 slice-start
  125.7 4.7 %fusion.21 = f32[8,4096]{1,0:T(8,128)S(1)} fusion(bf16[1024,4096]{1,0:T(8,128)(2,1)} %param.8, f32[1024,8]{0,1:T(8,128)S(1)} %multiply_add_fusion), kind=kOutput, calls=%fused_computation.35 | convolution fusion | flops 67117056 | bytes 8552448 | tf_op jit(solution)/shard_map/dot_general | solution.py:22
  130.4 0.0 copy-start.7
  130.4 0.0 slice-start.1
  130.4 4.7 %fusion.13 = f32[256,128]{1,0:T(8,128)S(1)} fusion(f32[8,4096]{1,0:T(8,128)S(1)} %fusion.21, bf16[1024,4096]{1,0:T(8,128)(2,1)} %param.8, f32[1024,8]{0,1:T(8,128)S(1)} %multiply_add_fusion), kind=kOutput, calls=%fused_computation.15 | convolution fusion | flops 67174400 | bytes 8683520 | tf_op jit(solution)/shard_map/dot_general | solution.py:22
  135.1 0.0 copy-done.7
  135.2 0.5 fusion.9
  135.7 0.0 slice-done
  135.7 0.0 slice-done.1
  135.8 3.5 %convolution_bitcast_fusion = f32[4096,128]{1,0:T(8,128)S(1)} fusion(bf16[1024,128]{0,1:T(8,128)(2,1)S(1)} %get-tuple-element.20, bf16[1024,4096]{1,0:T(8,128)(2,1)S(1)} %bitcast.52), kind=kOutput, calls=%fused_computation.1 | convolution fusion | flops 1073741824 | bytes 10747904 | tf_op jit(solution)/shard_map/dot_general | solution.py:22
  139.2 1.7 pad_maximum_fusion.part_ref
  141.0 39.0 %reduce_clip.1 = (f32[4096,128]{1,0:T(8,128)}, f32[128,1024]{1,0:T(8,128)}, f32[8,4096]{1,0:T(8,128)}) custom-call(f32[5376,128]{1,0:T(8,128)} %pad_maximum_fusion.part_ref), custom_call_target="tpu_custom_call" | custom-call | tf_op jit(solution)/shard_map/reduce_clip/pallas_call | solution.py:186
  181.3 0.0 copy-start.6
  181.3 0.0 copy-start.8
  181.3 0.0 copy-start.4
  181.3 0.0 copy-start.1
  181.4 12.7 %fusion.26 = f32[1024,1024]{1,0:T(8,128)S(1)} fusion(bf16[1024,4096]{1,0:T(8,128)(2,1)} %param.8, bf16[4096,1024]{1,0:T(8,128)(2,1)} %param.9), kind=kOutput, calls=%fused_computation.48 | convolution fusion | flops 8589934592 | bytes 20971520 | tf_op jit(solution)/shard_map/dot_general | solution.py:221
  194.1 0.0 copy-done.6
  194.1 0.0 copy-done.8
  194.1 0.0 copy-start.9
  194.1 0.0 copy-start.10
  194.1 2.1 %add_convert_fusion.1 = bf16[1024,1024]{1,0:T(8,128)(2,1)} fusion(f32[1024,1024]{1,0:T(8,128)S(1)} %fusion.26, bf16[1024,128]{0,1:T(8,128)(2,1)S(1)} %copy-done.8, bf16[128,1024]{1,0:T(8,128)(2,1)S(1)} %copy-done.6), kind=kOutput, calls=%fused_computation.3 | convolution fusion | flops 271581184 | bytes 6815744 | tf_op jit(solution)/shard_map/dot_general | solution.py:229
  196.2 0.0 copy-done.4
  196.2 1.3 copy.23
  197.5 0.0 copy-done.9
  197.5 0.8 copy.24
  198.3 0.0 copy-done.10
  198.3 0.7 copy.25
  199.0 0.0 copy-done.1
  (8 shorter events, 0.1 us)
Async XLA Ops:
  0.6 6.0 %copy-start = (bf16[4096,128]{1,0:T(8,128)(2,1)S(1)}, bf16[4096,128]{1,0:T(8,128)(2,1)}, u32[]{:S(2)}) copy-start(bf16[4096,128]{1,0:T(8,128)(2,1)} %param.10) | copy-start | bytes 3145732
  0.6 6.1 %copy-start.2 = (bf16[1024,4096]{1,0:T(8,128)(2,1)S(1)}, bf16[1024,4096]{1,0:T(8,128)(2,1)}, u32[]{:S(2)}) copy-start(bf16[1024,4096]{1,0:T(8,128)(2,1)} %param.8) | copy-start | bytes 25165828
  0.7 5.9 %copy-start.11 = (s32[1024]{0:T(1024)S(1)}, s32[1024]{0:T(1024)}, u32[]{:S(2)}) copy-start(s32[1024]{0:T(1024)} %param.7) | copy-start | bytes 12292
  6.5 3.2 %copy-start.3 = (bf16[1024,1024]{1,0:T(8,128)(2,1)S(1)}, bf16[1024,1024]{1,0:T(8,128)(2,1)}, u32[]{:S(2)}) copy-start(bf16[1024,1024]{1,0:T(8,128)(2,1)} %param.13) | copy-start | bytes 6291460
  6.5 3.2 %copy-start.5 = (bf16[128,1024]{1,0:T(8,128)(2,1)S(1)}, bf16[128,1024]{1,0:T(8,128)(2,1)}, u32[]{:S(2)}) copy-start(bf16[128,1024]{1,0:T(8,128)(2,1)} %param.11) | copy-start | bytes 786436
  125.7 10.0 %slice-start = ((s8[8388608]{0:T(1024)(128)(4,1)}), s8[4194304]{0:T(1024)(128)(4,1)S(1)}, s32[]{:S(2)}) async-start(s8[8388608]{0:T(1024)(128)(4,1)} %bitcast.51), calls=%async_computation | async-start | bytes 8388608
  130.4 4.7 %copy-start.7 = (bf16[1024,128]{0,1:T(8,128)(2,1)S(1)}, bf16[1024,128]{0,1:T(8,128)(2,1)}, u32[]{:S(2)}) copy-start(bf16[1024,128]{0,1:T(8,128)(2,1)} %get-tuple-element.22) | copy-start | bytes 786436
  130.4 5.3 %slice-start.1 = ((s8[8388608]{0:T(1024)(128)(4,1)}), s8[4194304]{0:T(1024)(128)(4,1)S(1)}, s32[]{:S(2)}) async-start(s8[8388608]{0:T(1024)(128)(4,1)} %bitcast.51), calls=%async_computation.1 | async-start | bytes 8388608
  181.3 12.8 %copy-start.6 = (bf16[128,1024]{1,0:T(8,128)(2,1)S(1)}, bf16[128,1024]{1,0:T(8,128)(2,1)}, u32[]{:S(2)}) copy-start(bf16[128,1024]{1,0:T(8,128)(2,1)} %param.11) | copy-start | bytes 786436
  181.3 12.8 %copy-start.8 = (bf16[1024,128]{0,1:T(8,128)(2,1)S(1)}, bf16[1024,128]{0,1:T(8,128)(2,1)}, u32[]{:S(2)}) copy-start(bf16[1024,128]{0,1:T(8,128)(2,1)} %get-tuple-element.22) | copy-start | bytes 786436
  181.3 14.9 %copy-start.4 = (f32[4096,128]{1,0:T(8,128)S(1)}, f32[4096,128]{1,0:T(8,128)}, u32[]{:S(2)}) copy-start(f32[4096,128]{1,0:T(8,128)} %get-tuple-element.42) | copy-start | bytes 6291460
  181.3 17.6 %copy-start.1 = (bf16[4096,128]{1,0:T(8,128)(2,1)S(1)}, bf16[4096,128]{1,0:T(8,128)(2,1)}, u32[]{:S(2)}) copy-start(bf16[4096,128]{1,0:T(8,128)(2,1)} %param.10) | copy-start | bytes 3145732
  194.1 3.4 %copy-start.9 = (f32[128,1024]{1,0:T(8,128)S(1)}, f32[128,1024]{1,0:T(8,128)}, u32[]{:S(2)}) copy-start(f32[128,1024]{1,0:T(8,128)} %get-tuple-element.43) | copy-start | bytes 1572868
  194.1 4.2 %copy-start.10 = (f32[8,4096]{1,0:T(8,128)S(1)}, f32[8,4096]{1,0:T(8,128)}, u32[]{:S(2)}) copy-start(f32[8,4096]{1,0:T(8,128)} %get-tuple-element.12) | copy-start | bytes 393220

commit v2 on v0

v2 whole, which is shorter than its diff:
```python
import functools
import math

import jax
import jax.numpy as jnp
from jax import lax
from jax.experimental import pallas as pl
from jax.experimental.pallas import tpu as pltpu
from jax.sharding import Mesh
from jax.sharding import PartitionSpec as P

AXES = ("dp_0", "dp_1", "dp_2")
CORE = "dp_3"
DP = AXES + (CORE,)
MESH = pl.DeviceIdType.MESH
SIDE = 4
LANES = 128
CHUNK = 256
BF16 = jnp.bfloat16
F32 = jnp.float32


def dot(first, second):
    return jnp.dot(first, second, preferred_element_type=F32)


def right_dot(first, second):
    return lax.dot_general(first, second, (((1,), (1,)), ((), ())), preferred_element_type=F32)


def ring_peer(axis, distance):
    return {axis: lax.rem(lax.axis_index(axis) + distance, SIDE)}


def span(start, size, unit=8):
    return pl.ds(pl.multiple_of(start, unit), size)


class Piece:
    def __init__(self, index, base, rows):
        self.index, self.base, self.rows = index, base, rows
        self.half, self.quarter, self.last = rows // 2, rows // 8, rows // 32
        self.first, self.second, self.third = (AXES[(index + step) % 3] for step in range(3))


class Exchange:
    def __init__(self, part, total, halves, firsts, seconds, thirds, send, recv):
        self.part, self.total = part, total
        self.halves, self.firsts, self.seconds, self.thirds = halves, firsts, seconds, thirds
        self.send, self.recv = send, recv
        self.core = lax.axis_index(CORE)

    def half_at(self, piece, core):
        return piece.base + core * piece.half

    def quarter_at(self, piece, place):
        return self.half_at(piece, self.core) + place * piece.quarter

    def last_at(self, piece, place, second):
        return self.quarter_at(piece, place) + second * piece.last

    def copies(self, phase, piece):
        one, two = lax.axis_index(piece.first), lax.axis_index(piece.second)

        def copy(source, target, slot, device):
            return pltpu.make_async_remote_copy(
                src_ref=source,
                dst_ref=target,
                send_sem=self.send.at[phase, piece.index, slot],
                recv_sem=self.recv.at[phase, piece.index, slot],
                device_id=device,
                device_id_type=MESH,
            )

        if phase == 0:
            source = self.part.at[span(self.half_at(piece, 1 - self.core), piece.half)]
            target = self.halves.at[pl.ds(piece.base // 2, piece.half)]
            return [copy(source, target, 0, {CORE: 1 - self.core})]
        if phase == 6:
            here = self.total.at[span(self.half_at(piece, self.core), piece.half)]
            return [copy(here, here, 0, {CORE: 1 - self.core})]
        made = []
        for distance in (1, 2, 3):
            slot = distance - 1
            if phase == 1:
                place = lax.rem(one + distance, SIDE)
                source = self.part.at[span(self.quarter_at(piece, place), piece.quarter)]
                target = self.firsts.at[slot, pl.ds(piece.base // 8, piece.quarter)]
                axis = piece.first
            elif phase == 2:
                place = lax.rem(two + distance, SIDE)
                source = self.part.at[span(self.last_at(piece, one, place), piece.last)]
                target = self.seconds.at[slot, pl.ds(piece.base // 32, piece.last)]
                axis = piece.second
            elif phase == 3:
                source = self.part.at[span(self.last_at(piece, one, two), piece.last)]
                target = self.thirds.at[lax.axis_index(piece.third), pl.ds(piece.base // 32, piece.last)]
                axis = piece.third
            elif phase == 4:
                source = self.total.at[span(self.last_at(piece, one, two), piece.last)]
                target, axis = source, piece.second
            else:
                source = self.total.at[span(self.quarter_at(piece, one), piece.quarter)]
                target, axis = source, piece.first
            made.append(copy(source, target, slot, ring_peer(axis, distance)))
        return made

    def start(self, phase, piece):
        for copy in self.copies(phase, piece):
            copy.start()

    def finish(self, phase, piece):
        for copy in self.copies(phase, piece):
            copy.wait()
        one, two = lax.axis_index(piece.first), lax.axis_index(piece.second)
        if phase == 0:
            here = span(self.half_at(piece, self.core), piece.half)
            self.part[here] = self.part[here] + self.halves[pl.ds(piece.base // 2, piece.half)]
        elif phase == 1:
            here = span(self.quarter_at(piece, one), piece.quarter)
            there = pl.ds(piece.base // 8, piece.quarter)
            got = self.firsts
            self.part[here] = (self.part[here] + got[0, there]) + (got[1, there] + got[2, there])
        elif phase == 2:
            here = span(self.last_at(piece, one, two), piece.last)
            there = pl.ds(piece.base // 32, piece.last)
            got = self.seconds
            self.part[here] = (self.part[here] + got[0, there]) + (got[1, there] + got[2, there])
        elif phase == 3:
            here = span(self.last_at(piece, one, two), piece.last)
            there = pl.ds(piece.base // 32, piece.last)
            got = self.thirds
            got[lax.axis_index(piece.third), there] = self.part[here]
            self.total[here] = (got[0, there] + got[1, there]) + (got[2, there] + got[3, there])

    def step(self, phase, piece):
        self.finish(phase, piece)
        self.start(phase + 1, piece)


class Statistics:
    def __init__(self, tiles, wide, narrow, send, recv):
        self.tiles, self.wide, self.narrow = tiles, wide, narrow
        self.send, self.recv = send, recv

    def copies(self, stage):
        made = []
        for distance in range(1, 8 if stage == 0 else SIDE):
            if stage == 0:
                mine = lax.axis_index(CORE) * SIDE + lax.axis_index(AXES[0])
                other = lax.rem(mine + distance, 8)
                device = {CORE: lax.div(other, SIDE), AXES[0]: lax.rem(other, SIDE)}
                target = self.wide.at[mine]
            else:
                device = ring_peer(AXES[stage], distance)
                target = self.narrow.at[stage - 1, lax.axis_index(AXES[stage])]
            made.append(
                pltpu.make_async_remote_copy(
                    src_ref=self.tiles.at[stage],
                    dst_ref=target,
                    send_sem=self.send.at[stage, distance - 1],
                    recv_sem=self.recv.at[stage, distance - 1],
                    device_id=device,
                    device_id_type=MESH,
                )
            )
        return made

    def start(self, stage):
        for copy in self.copies(stage):
            copy.start()

    def finish(self, stage):
        for copy in self.copies(stage):
            copy.wait()
        if stage == 0:
            self.wide[lax.axis_index(CORE) * SIDE + lax.axis_index(AXES[0])] = self.tiles[0]
            got = [self.wide[place] for place in range(8)]
        else:
            self.narrow[stage - 1, lax.axis_index(AXES[stage])] = self.tiles[stage]
            got = [self.narrow[stage - 1, place] for place in range(SIDE)]
        total = got[0]
        for other in got[1:]:
            total = total + other
        self.tiles[stage + 1] = total


def peers():
    core, x = lax.axis_index(CORE), lax.axis_index(AXES[0])
    found = [{CORE: 1 - core}]
    for distance in (1, 2, 3):
        found.append({CORE: 1 - core, AXES[0]: lax.rem(x + distance, SIDE)})
        found += [ring_peer(axis, distance) for axis in AXES]
    return found


def kernel(
    sizes,
    ids_hbm, tokens_hbm, frozen_hbm, down_hbm, up_hbm, gate_hbm, upstream_hbm,
    projected_ref, input_ref, down_ref, up_ref, gate_ref, stats_ref,
    ids, tokens, frozen, sides, up, gate, masked,
    low, prob, plain, weighted, grads, grads_t, weighted_t, gate_t,
    part, total, halves, firsts, seconds, thirds, tiles, wide, narrow,
    load_sem, token_sem, send, recv, stat_send, stat_recv,
):
    rows, width, outputs, ranks, experts = sizes
    rank = ranks // experts
    scale = 1.0 / rank
    chunks = rows // CHUNK
    up_base = width
    gate_base = width + outputs
    pieces = (Piece(0, 0, 1792), Piece(1, 1792, 1792), Piece(2, 3584, gate_base - 3584), Piece(3, gate_base, width * experts // LANES))
    exchange = Exchange(part, total, halves, firsts, seconds, thirds, send, recv)
    statistics = Statistics(tiles, wide, narrow, stat_send, stat_recv)

    barrier = pltpu.get_barrier_semaphore()
    greeted = peers()
    for peer in greeted:
        pl.semaphore_signal(barrier, inc=1, device_id=peer, device_id_type=MESH)

    def load(source, target, slot):
        return pltpu.make_async_copy(source, target, load_sem.at[slot])

    def token_load(chunk):
        here = span(chunk * CHUNK, CHUNK, CHUNK)
        return pltpu.make_async_copy(tokens_hbm.at[here], tokens.at[here], token_sem.at[chunk])

    gate_load = load(gate_hbm, gate, 0)
    ids_load = load(ids_hbm, ids, 1)
    down_load = load(down_hbm, sides.at[:, pl.ds(0, ranks)], 2)
    up_load = load(up_hbm, up, 3)
    upstream_load = load(upstream_hbm, masked, 4)
    frozen_load = load(frozen_hbm, frozen, 5)
    gate_load.start()
    ids_load.start()
    down_load.start()
    for chunk in range(chunks):
        token_load(chunk).start()
    up_load.start()
    upstream_load.start()
    frozen_load.start()

    gate_load.wait()

    @pl.loop(0, width // 512)
    def _(block):
        here = span(block * 512, 512, 512)
        row = gate[:, here].astype(F32)
        tall = jnp.concatenate([jnp.broadcast_to(row[e : e + 1], (rank, 512)) for e in range(experts)], axis=0)
        sides[here, ranks : 2 * ranks] = tall.T.astype(BF16)

    ids_load.wait()
    live_rows = jnp.sum(jnp.sum((ids[...] != 0).astype(F32), axis=1, keepdims=True), axis=0, keepdims=True)

    def live_of(chunk):
        row = lax.broadcasted_iota(jnp.int32, (CHUNK, LANES), 0) + chunk * CHUNK
        return (row.astype(F32) < live_rows).astype(F32)

    def lane_sum(value):
        return jnp.sum(value, axis=1, keepdims=True)

    tiles[0] = jnp.zeros((8, LANES), F32)
    down_load.wait()

    @pl.loop(0, chunks)
    def _(chunk):
        here = span(chunk * CHUNK, CHUNK, CHUNK)
        token_load(chunk).wait()
        both = dot(tokens[here], sides[...])
        low[here] = both[:, :ranks].astype(BF16)
        logits = both[:, ranks:]
        shifted = logits - jnp.max(logits, axis=1, keepdims=True)
        raised = jnp.exp(shifted)
        mass = lane_sum(raised) * scale
        share = raised / mass
        logp = shifted - jnp.log(mass)
        entropy = -lane_sum(share * logp) * scale
        alive = live_of(chunk)
        prob[here] = share
        plain[here] = 50.0 * alive * share * (logp + entropy)
        tiles[0, 0:1] += jnp.sum(alive * share, axis=0, keepdims=True)
        tiles[0, 1:2] += jnp.sum(alive * entropy, axis=0, keepdims=True)
        tiles[0, 2:3] += jnp.sum(alive, axis=0, keepdims=True)

    pl.semaphore_wait(barrier, len(greeted))
    statistics.start(0)

    up_load.wait()
    upstream_load.wait()
    group = lax.broadcasted_iota(jnp.int32, (2 * ranks, ranks), 0) % ranks // rank
    member = lax.broadcasted_iota(jnp.int32, (2 * ranks, ranks), 1) // rank
    blocks = (group == member).astype(F32).astype(BF16)

    @pl.loop(0, chunks)
    def _(chunk):
        here = span(chunk * CHUNK, CHUNK, CHUNK)
        alive = live_of(chunk)[:, 0:1]
        mine = jnp.where(alive > 0.0, masked[here].astype(F32), 0.0).astype(BF16)
        masked[here] = mine
        back = right_dot(mine, up[...])
        share = prob[here]
        below = low[here].astype(F32)
        heavy = (below * share).astype(BF16).astype(F32) * 2.0
        steep = (2.0 * share * back).astype(BF16)
        weighted[here] = heavy.astype(BF16)
        grads[here, 0:ranks] = steep
        grads_t[:, here] = steep.astype(F32).T.astype(BF16)
        weighted_t[:, here] = heavy.T.astype(BF16)
        product = below * back
        upper = product.astype(BF16)
        lower = (product - upper.astype(F32)).astype(BF16)
        task = 2.0 * dot(jnp.concatenate([upper, lower], axis=1), blocks)
        plain[here] += share * (task - lane_sum(share * task) * scale)

    statistics.finish(0)
    statistics.start(1)

    def down_blocks(first, last):
        @pl.loop(first, last)
        def _(block):
            here = span(block * 256, 256, 256)
            part[here] = dot(grads_t[...], tokens[:, here]).T

    down_blocks(0, 7)
    exchange.start(0, pieces[0])
    statistics.finish(1)
    statistics.start(2)
    down_blocks(7, 14)
    exchange.start(0, pieces[1])
    exchange.step(0, pieces[0])
    down_blocks(14, 16)

    @pl.loop(0, outputs // 256)
    def _(block):
        found = dot(weighted_t[...], masked[:, span(block * 256, 256, 256)])
        part[span(up_base + block * 256, LANES, LANES)] = found[:, :LANES]
        part[span(up_base + block * 256 + LANES, LANES, LANES)] = found[:, LANES:]

    exchange.start(0, pieces[2])
    exchange.step(0, pieces[1])
    statistics.finish(2)
    load_all, live_all = tiles[3, 0:1], tiles[3, 2:3]
    push = (2.0 * experts * 100.0) / live_all
    lane = lax.broadcasted_iota(jnp.int32, (CHUNK, LANES), 1)
    pick_from = lax.broadcasted_iota(jnp.int32, (ranks, ranks), 0)
    pick_to = lax.broadcasted_iota(jnp.int32, (ranks, ranks), 1)
    pick = (pick_from == (pick_to % experts) * rank + pick_to // experts).astype(F32)
    pick = jnp.where(pick_to < 2 * experts, pick, 0.0).astype(BF16)

    @pl.loop(0, chunks)
    def _(chunk):
        here = span(chunk * CHUNK, CHUNK, CHUNK)
        share = prob[here]
        slope = share * (load_all - lane_sum(share * load_all) * scale)
        whole = plain[here] + push * live_of(chunk) * slope
        upper = whole.astype(BF16).astype(F32)
        place = lane % rank
        packed = jnp.where(place == 0, upper, jnp.where(place == 1, whole - upper, 0.0)).astype(BF16)
        grads[here, ranks : 2 * ranks] = packed
        gate_t[:, here] = dot(packed, pick).T[: 2 * experts].astype(BF16)

    @pl.loop(0, width // 512)
    def _(block):
        found = dot(gate_t[...], tokens[:, span(block * 512, 512, 512)])
        found = found[:experts] + found[experts:]
        for piece in range(4):
            here = span(gate_base + (block * 4 + piece) * experts, experts)
            part[here] = found[:, piece * LANES : (piece + 1) * LANES]

    exchange.start(0, pieces[3])
    exchange.step(0, pieces[2])

    def base_blocks(first, last):
        @pl.loop(first, last)
        def _(block):
            tall = span((block % 2) * (rows // 2), rows // 2, rows // 2)
            here = span((block // 2) * 256, 256, 256)
            found = dot(tokens[tall], frozen[:, here]) + dot(weighted[tall], up[:, here])
            projected_ref[tall, here] = found.astype(BF16)

    def input_blocks(first, last):
        @pl.loop(first, last)
        def _(block):
            here = span(block * 256, 256, 256)
            found = right_dot(masked[...], frozen[here]) + right_dot(grads[...], sides[here])
            input_ref[:, here] = found.astype(BF16)

    def step_all(phase):
        for piece in pieces[:3]:
            exchange.step(phase, piece)

    frozen_load.wait()
    base_blocks(0, 2)
    exchange.step(0, pieces[3])
    base_blocks(2, 5)
    step_all(1)
    base_blocks(5, 8)
    exchange.step(1, pieces[3])
    step_all(2)
    input_blocks(0, 4)
    exchange.step(2, pieces[3])
    step_all(3)
    input_blocks(4, 8)
    exchange.step(3, pieces[3])
    step_all(4)
    input_blocks(8, 12)
    exchange.step(4, pieces[3])
    input_blocks(12, 16)
    step_all(5)
    exchange.step(5, pieces[3])
    for piece in pieces:
        exchange.finish(6, piece)

    every = width + outputs + width * experts // LANES
    squares = jnp.zeros((8, LANES), F32)

    def add_squares(block, found):
        for piece in range(4):
            value = total[span((block * 4 + piece) * 8, 8)]
            found = found + value * value
        return found

    squares = lax.fori_loop(0, every // 32, add_squares, squares)
    norm = jnp.sqrt(jnp.sum(lane_sum(squares), axis=0, keepdims=True))
    limit = math.sqrt(every * LANES)
    factor = jnp.minimum(1.0, limit / norm)

    @pl.loop(0, width // 256)
    def _(block):
        here = span(block * 256, 256, 256)
        down_ref[here] = total[here] * factor

    for block in range(outputs // LANES):
        up_ref[:, block * LANES : (block + 1) * LANES] = total[up_base + block * LANES : up_base + (block + 1) * LANES] * factor
    for block in range(width // LANES):
        here = gate_base + block * experts
        gate_ref[:, block * LANES : (block + 1) * LANES] = total[here : here + experts] * factor

    to = lax.broadcasted_iota(jnp.int32, (8, LANES), 1)
    which = lax.broadcasted_iota(jnp.int32, (8, LANES), 0)
    mean = tiles[3] / live_all
    column = lane_sum(jnp.where(to == which * rank, jnp.broadcast_to(mean[0:1], (8, LANES)), 0.0))
    load_row = jnp.sum(jnp.where(to == which, jnp.broadcast_to(column, (8, LANES)), 0.0), axis=0, keepdims=True)
    stats_ref[...] = jnp.where(which == 0, jnp.broadcast_to(load_row, (8, LANES)), jnp.broadcast_to(mean[1:2], (8, LANES)))


def on_device(token_ids, tokens, frozen_weight, adapter_down, adapter_up, gate_weight, upstream):
    rows, width = tokens.shape
    ranks, outputs = adapter_up.shape
    experts = gate_weight.shape[1]
    every = width + outputs + width * experts // LANES
    anywhere = pl.BlockSpec(memory_space=pl.ANY)
    vmem = pl.BlockSpec(memory_space=pltpu.VMEM)
    found = pl.pallas_call(
        functools.partial(kernel, (rows, width, outputs, ranks, experts)),
        out_shape=(
            pltpu.VMEM((rows, outputs), BF16),
            pltpu.VMEM((rows, width), BF16),
            pltpu.VMEM((width, ranks), F32),
            pltpu.VMEM((ranks, outputs), F32),
            pltpu.VMEM((experts, width), F32),
            pltpu.VMEM((8, LANES), F32),
        ),
        in_specs=[anywhere] * 7,
        out_specs=(vmem,) * 6,
        scratch_shapes=[
            pltpu.VMEM((rows // LANES, LANES), jnp.int32),
            pltpu.VMEM((rows, width), BF16),
            pltpu.VMEM((width, outputs), BF16),
            pltpu.VMEM((width, 2 * ranks), BF16),
            pltpu.VMEM((ranks, outputs), BF16),
            pltpu.VMEM((experts, width), BF16),
            pltpu.VMEM((rows, outputs), BF16),
            pltpu.VMEM((rows, ranks), BF16),
            pltpu.VMEM((rows, ranks), F32),
            pltpu.VMEM((rows, ranks), F32),
            pltpu.VMEM((rows, ranks), BF16),
            pltpu.VMEM((rows, 2 * ranks), BF16),
            pltpu.VMEM((ranks, rows), BF16),
            pltpu.VMEM((ranks, rows), BF16),
            pltpu.VMEM((2 * experts, rows), BF16),
            pltpu.VMEM((every, LANES), F32),
            pltpu.VMEM((every, LANES), F32),
            pltpu.VMEM((every // 2, LANES), F32),
            pltpu.VMEM((3, every // 8, LANES), F32),
            pltpu.VMEM((3, every // 32, LANES), F32),
            pltpu.VMEM((4, every // 32, LANES), F32),
            pltpu.VMEM((4, 8, LANES), F32),
            pltpu.VMEM((8, 8, LANES), F32),
            pltpu.VMEM((2, SIDE, 8, LANES), F32),
            pltpu.SemaphoreType.DMA((6,)),
            pltpu.SemaphoreType.DMA((rows // CHUNK,)),
            pltpu.SemaphoreType.DMA((7, 4, 3)),
            pltpu.SemaphoreType.DMA((7, 4, 3)),
            pltpu.SemaphoreType.DMA((3, 7)),
            pltpu.SemaphoreType.DMA((3, 7)),
        ],
        compiler_params=pltpu.CompilerParams(
            collective_id=0, has_side_effects=True, vmem_limit_bytes=48 * 1024 * 1024
        ),
        name="step",
    )(token_ids.reshape(rows // LANES, LANES), tokens, frozen_weight, adapter_down, adapter_up, gate_weight.T, upstream)
    projected, input_grad, down, up, gate, stats = found
    return projected, input_grad, down, up, gate.T, stats[0, :experts], stats[1, 0]


def solution(mesh):
    torus = Mesh(mesh.devices.reshape(4, 4, 4, 2), DP)
    return jax.shard_map(
        on_device,
        mesh=torus,
        in_specs=(P(DP), P(DP, None), P(), P(), P(), P(), P(DP, None)),
        out_specs=(P(DP, None), P(DP, None), P(), P(), P(), P(), P()),
        check_vma=False,
    )
```

time: 243 us -> 68.5 us (0.28)
  waiting for transfers between devices: 89.6 us -> 0 us
  matrix products: 79.3 us -> 0 us
  Pallas kernels: 0 us -> 59.3 us
  blocking collectives: 39.1 us -> 0 us
  between operations: 19.4 us -> 0.65 us
  other arithmetic: 13.5 us -> 0 us
  local copies, waits for them, and re-layouts: 2.14 us -> 8.51 us
    psum x1 -> x0, waiting for transfers between devices: 89.6 us -> none  [reduce_clip(): summed = lax.psum((terms[0], terms[1], terms[2]), DP)]
    dot_general x12 -> x0, matrix products: 79.3 us -> none  [the longest x3 31.5 us: right_dot(): lax.dot_general(first, second, (((1,), (1,)), ((), ())), preferred_elemen...]
    pallas_call x0 -> x1, Pallas kernels: none -> 59.3 us  [on_device(): pl.pallas_call(functools.partial(kernel, (rows, width, outputs, ranks, ex...]
    psum x4 -> x0, blocking collectives: 39.1 us -> none  [over_axes(): x = lax.psum(x, axis)]
    reduce_sum x8 -> x0, other arithmetic: 6.98 us -> none  [the longest x1 2.73 us: reduce_clip(): jnp.sum(grads[0] * grads[0]) + jnp.sum(grads[1] * grads[1])]
    unnamed x23 -> x5, local copies, waits for them, and re-layouts: 2.14 us -> 7.48 us
    mul x5 -> x0, other arithmetic: 5.24 us -> none  [the longest x3 5.23 us: reduce_clip(): return (grads[0] * factor, grads[1] * factor, grads[2] * factor)]
  transfers between devices with their start and end apart: 1 -> 0, of which waited for: 1 -> 0; matrix products, arithmetic and copies ran while one was open for 23% -> 0% of each run, Pallas kernels for 0% -> 0%
where the time goes in v2:
time: 68.5 us; the launch traced here: 68.4 us
  Pallas kernels  59.3 us (87%)
  local copies, waits for them, and re-layouts  8.51 us (12%)
    pallas_call x1, Pallas kernels, on_device(): pl.pallas_call(functools.partial(kernel, (rows, width, outputs, ranks, ex...  59.3 us
    unnamed x5, local copies, waits for them, and re-layouts  7.48 us

profile of v2, /device:TPU:1, one launch (start us, length us, event | category | flops | bytes accessed | tf_op | source)
XLA Modules:
  0.0 68.4 jit_solution(14336732126106475525)
XLA Ops:
  0.6 59.3 %step.1 = (bf16[1024,1024]{1,0:T(8,128)(2,1)S(1)}, bf16[1024,4096]{1,0:T(8,128)(2,1)S(1)}, f32[4096,128]{1,0:T(8,128)S(1)}, f32[128,1024]{1,0:T(8,128)S(1)}, f32...) custom-call(s32[8,128]{1,0:T(8,128)} %bitcast.8, bf16[1024,4096]{1,0:T(8,128)(2,1)} %tokens_hbm.1, ...), custom_call_target="tpu_custom_call" | custom-call | tf_op jit(solution)/shard_map/step/pallas_call | solution.py:454
  59.9 0.5 slice.7
  60.4 1.3 %copy.19 = bf16[1024,1024]{1,0:T(8,128)(2,1)} copy(bf16[1024,1024]{1,0:T(8,128)(2,1)S(1)} %get-tuple-element.19) | data formatting | bytes 4194304
  61.7 0.5 slice_bitcast_fusion
  62.2 0.7 copy.23
  62.9 0.8 %copy.22 = f32[128,1024]{1,0:T(8,128)} copy(f32[128,1024]{1,0:T(8,128)S(1)} %get-tuple-element.22) | data formatting | bytes 1048576
  63.7 1.3 %copy.21 = f32[4096,128]{1,0:T(8,128)} copy(f32[4096,128]{1,0:T(8,128)S(1)} %get-tuple-element.21) | data formatting | bytes 4194304
  65.0 3.4 %copy.20 = bf16[1024,4096]{1,0:T(8,128)(2,1)} copy(bf16[1024,4096]{1,0:T(8,128)(2,1)S(1)} %get-tuple-element.20) | data formatting | bytes 16777216

commit v3 on v2

--- a/solution.py
+++ b/solution.py
@@ -197,10 +197,10 @@
 def kernel(
     sizes,
     ids_hbm, tokens_hbm, frozen_hbm, down_hbm, up_hbm, gate_hbm, upstream_hbm,
-    projected_ref, input_ref, down_ref, up_ref, gate_ref, stats_ref,
+    projected_ref, input_ref, total, tiles,
     ids, tokens, frozen, sides, up, gate, masked,
-    low, prob, plain, weighted, grads, grads_t, weighted_t, gate_t,
-    part, total, halves, firsts, seconds, thirds, tiles, wide, narrow,
+    low, prob, plain, turned, weighted, grads, grads_t, weighted_t, gate_t,
+    part, halves, firsts, seconds, thirds, wide, narrow,
     load_sem, token_sem, send, recv, stat_send, stat_recv,
 ):
     rows, width, outputs, ranks, experts = sizes
@@ -236,9 +236,6 @@
     down_load.start()
     for chunk in range(chunks):
         token_load(chunk).start()
-    up_load.start()
-    upstream_load.start()
-    frozen_load.start()
 
     gate_load.wait()
 
@@ -266,6 +263,16 @@
     def _(chunk):
         here = span(chunk * CHUNK, CHUNK, CHUNK)
         token_load(chunk).wait()
+
+        @pl.when(chunk == 1)
+        def _():
+            up_load.start()
+            upstream_load.start()
+
+        @pl.when(chunk == 3)
+        def _():
+            frozen_load.start()
+
         both = dot(tokens[here], sides[...])
         low[here] = both[:, :ranks].astype(BF16)
         logits = both[:, ranks:]
@@ -287,9 +294,6 @@
 
     up_load.wait()
     upstream_load.wait()
-    group = lax.broadcasted_iota(jnp.int32, (2 * ranks, ranks), 0) % ranks // rank
-    member = lax.broadcasted_iota(jnp.int32, (2 * ranks, ranks), 1) // rank
-    blocks = (group == member).astype(F32).astype(BF16)
 
     @pl.loop(0, chunks)
     def _(chunk):
@@ -299,45 +303,73 @@
         masked[here] = mine
         back = right_dot(mine, up[...])
         share = prob[here]
-        below = low[here].astype(F32)
-        heavy = (below * share).astype(BF16).astype(F32) * 2.0
+        heavy = (low[here].astype(F32) * share).astype(BF16).astype(F32) * 2.0
         steep = (2.0 * share * back).astype(BF16)
+        turned[here] = back
         weighted[here] = heavy.astype(BF16)
         grads[here, 0:ranks] = steep
         grads_t[:, here] = steep.astype(F32).T.astype(BF16)
         weighted_t[:, here] = heavy.T.astype(BF16)
-        product = below * back
+
+    def down_block(start, size):
+        here = pl.ds(start, size)
+        part[here] = dot(grads_t[...], tokens[:, here]).T
+
+    down_block(0, 896)
+    down_block(896, 896)
+    exchange.start(0, pieces[0])
+    down_block(1792, 896)
+    down_block(2688, 896)
+    exchange.start(0, pieces[1])
+    down_block(3584, 512)
+    found = dot(weighted_t[...], masked[...])
+    for block in range(outputs // LANES):
+        part[up_base + block * LANES : up_base + (block + 1) * LANES] = found[:, block * LANES : (block + 1) * LANES]
+    exchange.start(0, pieces[2])
+    exchange.step(0, pieces[0])
+    statistics.finish(0)
+    statistics.start(1)
+    group = lax.broadcasted_iota(jnp.int32, (2 * ranks, ranks), 0) % ranks // rank
+    member = lax.broadcasted_iota(jnp.int32, (2 * ranks, ranks), 1) // rank
+    blocks = (group == member).astype(F32).astype(BF16)
+
+    @pl.loop(0, chunks)
+    def _(chunk):
+        here = span(chunk * CHUNK, CHUNK, CHUNK)
+        share = prob[here]
+        product = low[here].astype(F32) * turned[here]
         upper = product.astype(BF16)
         lower = (product - upper.astype(F32)).astype(BF16)
         task = 2.0 * dot(jnp.concatenate([upper, lower], axis=1), blocks)
         plain[here] += share * (task - lane_sum(share * task) * scale)
 
-    statistics.finish(0)
-    statistics.start(1)
-
-    def down_blocks(first, last):
+    exchange.step(0, pieces[1])
+
+    def base_blocks(first, last):
         @pl.loop(first, last)
         def _(block):
-            here = span(block * 256, 256, 256)
-            part[here] = dot(grads_t[...], tokens[:, here]).T
-
-    down_blocks(0, 7)
-    exchange.start(0, pieces[0])
+            tall = span((block % 2) * (rows // 2), rows // 2, rows // 2)
+            here = span((block // 2) * 256, 256, 256)
+            found = dot(tokens[tall], frozen[:, here]) + dot(weighted[tall], up[:, here])
+            projected_ref[tall, here] = found.astype(BF16)
+
+    def input_blocks(first, last):
+        @pl.loop(first, last)
+        def _(block):
+            here = span(block * 512, 512, 512)
+            found = right_dot(masked[...], frozen[here]) + right_dot(grads[...], sides[here])
+            input_ref[:, here] = found.astype(BF16)
+
+    def step_all(phase):
+        for piece in pieces[:3]:
+            exchange.step(phase, piece)
+
+    frozen_load.wait()
+    base_blocks(0, 1)
+    exchange.step(0, pieces[2])
     statistics.finish(1)
     statistics.start(2)
-    down_blocks(7, 14)
-    exchange.start(0, pieces[1])
-    exchange.step(0, pieces[0])
-    down_blocks(14, 16)
-
-    @pl.loop(0, outputs // 256)
-    def _(block):
-        found = dot(weighted_t[...], masked[:, span(block * 256, 256, 256)])
-        part[span(up_base + block * 256, LANES, LANES)] = found[:, :LANES]
-        part[span(up_base + block * 256 + LANES, LANES, LANES)] = found[:, LANES:]
-
-    exchange.start(0, pieces[2])
-    exchange.step(0, pieces[1])
+    base_blocks(1, 3)
     statistics.finish(2)
     load_all, live_all = tiles[3, 0:1], tiles[3, 2:3]
     push = (2.0 * experts * 100.0) / live_all
@@ -359,89 +391,86 @@
         grads[here, ranks : 2 * ranks] = packed
         gate_t[:, here] = dot(packed, pick).T[: 2 * experts].astype(BF16)
 
-    @pl.loop(0, width // 512)
+    @pl.loop(0, width // 1024)
     def _(block):
-        found = dot(gate_t[...], tokens[:, span(block * 512, 512, 512)])
+        found = dot(gate_t[...], tokens[:, span(block * 1024, 1024, 1024)])
         found = found[:experts] + found[experts:]
-        for piece in range(4):
-            here = span(gate_base + (block * 4 + piece) * experts, experts)
+        for piece in range(8):
+            here = span(gate_base + (block * 8 + piece) * experts, experts)
             part[here] = found[:, piece * LANES : (piece + 1) * LANES]
 
     exchange.start(0, pieces[3])
-    exchange.step(0, pieces[2])
-
-    def base_blocks(first, last):
-        @pl.loop(first, last)
-        def _(block):
-            tall = span((block % 2) * (rows // 2), rows // 2, rows // 2)
-            here = span((block // 2) * 256, 256, 256)
-            found = dot(tokens[tall], frozen[:, here]) + dot(weighted[tall], up[:, here])
-            projected_ref[tall, here] = found.astype(BF16)
-
-    def input_blocks(first, last):
-        @pl.loop(first, last)
-        def _(block):
-            here = span(block * 256, 256, 256)
-            found = right_dot(masked[...], frozen[here]) + right_dot(grads[...], sides[here])
-            input_ref[:, here] = found.astype(BF16)
-
-    def step_all(phase):
-        for piece in pieces[:3]:
-            exchange.step(phase, piece)
-
-    frozen_load.wait()
-    base_blocks(0, 2)
+    base_blocks(3, 4)
     exchange.step(0, pieces[3])
-    base_blocks(2, 5)
     step_all(1)
-    base_blocks(5, 8)
+    base_blocks(4, 7)
     exchange.step(1, pieces[3])
     step_all(2)
-    input_blocks(0, 4)
+    base_blocks(7, 8)
+    input_blocks(0, 1)
     exchange.step(2, pieces[3])
     step_all(3)
-    input_blocks(4, 8)
+    input_blocks(1, 3)
     exchange.step(3, pieces[3])
     step_all(4)
-    input_blocks(8, 12)
+    input_blocks(3, 5)
     exchange.step(4, pieces[3])
-    input_blocks(12, 16)
+    input_blocks(5, 8)
     step_all(5)
     exchange.step(5, pieces[3])
     for piece in pieces:
         exchange.finish(6, piece)
 
-    every = width + outputs + width * experts // LANES
-    squares = jnp.zeros((8, LANES), F32)
+
+def finish_kernel(
+    sizes,
+    projected, inputs, total, tiles,
+    projected_hbm, input_hbm, down_hbm, up_hbm, gate_hbm, load_ref, entropy_ref,
+    scaled, up, gate, sems,
+):
+    width, outputs, ranks, experts = sizes
+    rank = ranks // experts
+    every = total.shape[0]
+    quarter = width // 4
+    copies = [
+        pltpu.make_async_copy(inputs, input_hbm, sems.at[0]),
+        pltpu.make_async_copy(projected, projected_hbm, sems.at[1]),
+    ]
+    for copy in copies:
+        copy.start()
 
     def add_squares(block, found):
-        for piece in range(4):
-            value = total[span((block * 4 + piece) * 8, 8)]
-            found = found + value * value
-        return found
-
-    squares = lax.fori_loop(0, every // 32, add_squares, squares)
-    norm = jnp.sqrt(jnp.sum(lane_sum(squares), axis=0, keepdims=True))
-    limit = math.sqrt(every * LANES)
-    factor = jnp.minimum(1.0, limit / norm)
-
-    @pl.loop(0, width // 256)
-    def _(block):
-        here = span(block * 256, 256, 256)
-        down_ref[here] = total[here] * factor
-
+        value = total[span(block * 192, 192)]
+        return found + jnp.sum((value * value).reshape(6, 32, LANES), axis=0)
+
+    squares = lax.fori_loop(0, every // 192, add_squares, jnp.zeros((32, LANES), F32))
+    norm = jnp.sqrt(jnp.sum(jnp.sum(squares, axis=1, keepdims=True), axis=0, keepdims=True))
+    factor = jnp.minimum(1.0, math.sqrt(every * LANES) / norm)
+    for block in range(4):
+        here = pl.ds(block * quarter, quarter)
+        scaled[here] = total[here] * factor
+        copy = pltpu.make_async_copy(scaled.at[here], down_hbm.at[here], sems.at[2 + block])
+        copy.start()
+        copies.append(copy)
     for block in range(outputs // LANES):
-        up_ref[:, block * LANES : (block + 1) * LANES] = total[up_base + block * LANES : up_base + (block + 1) * LANES] * factor
+        here = width + block * LANES
+        up[:, block * LANES : (block + 1) * LANES] = total[here : here + LANES] * factor
+    copy = pltpu.make_async_copy(up, up_hbm, sems.at[6])
+    copy.start()
+    copies.append(copy)
     for block in range(width // LANES):
-        here = gate_base + block * experts
-        gate_ref[:, block * LANES : (block + 1) * LANES] = total[here : here + experts] * factor
-
-    to = lax.broadcasted_iota(jnp.int32, (8, LANES), 1)
-    which = lax.broadcasted_iota(jnp.int32, (8, LANES), 0)
-    mean = tiles[3] / live_all
-    column = lane_sum(jnp.where(to == which * rank, jnp.broadcast_to(mean[0:1], (8, LANES)), 0.0))
-    load_row = jnp.sum(jnp.where(to == which, jnp.broadcast_to(column, (8, LANES)), 0.0), axis=0, keepdims=True)
-    stats_ref[...] = jnp.where(which == 0, jnp.broadcast_to(load_row, (8, LANES)), jnp.broadcast_to(mean[1:2], (8, LANES)))
+        here = width + outputs + block * experts
+        gate[:, block * LANES : (block + 1) * LANES] = total[here : here + experts] * factor
+    copy = pltpu.make_async_copy(gate, gate_hbm, sems.at[7])
+    copy.start()
+    copies.append(copy)
+    mean = tiles[3] / tiles[3, 2:3]
+    lane = lax.broadcasted_iota(jnp.int32, (1, LANES), 1)
+    for expert in range(experts):
+        load_ref[expert] = jnp.sum(jnp.where(lane == expert * rank, mean[0:1], 0.0))
+    entropy_ref[0] = jnp.sum(jnp.where(lane == 0, mean[1:2], 0.0))
+    for copy in copies:
+        copy.wait()
 
 
 def on_device(token_ids, tokens, frozen_weight, adapter_down, adapter_up, gate_weight, upstream):
@@ -451,18 +480,17 @@
     every = width + outputs + width * experts // LANES
     anywhere = pl.BlockSpec(memory_space=pl.ANY)
     vmem = pl.BlockSpec(memory_space=pltpu.VMEM)
-    found = pl.pallas_call(
+    smem = pl.BlockSpec(memory_space=pltpu.SMEM)
+    held = pl.pallas_call(
         functools.partial(kernel, (rows, width, outputs, ranks, experts)),
         out_shape=(
             pltpu.VMEM((rows, outputs), BF16),
             pltpu.VMEM((rows, width), BF16),
-            pltpu.VMEM((width, ranks), F32),
-            pltpu.VMEM((ranks, outputs), F32),
-            pltpu.VMEM((experts, width), F32),
-            pltpu.VMEM((8, LANES), F32),
+            pltpu.VMEM((every, LANES), F32),
+            pltpu.VMEM((4, 8, LANES), F32),
         ),
         in_specs=[anywhere] * 7,
-        out_specs=(vmem,) * 6,
+        out_specs=(vmem,) * 4,
         scratch_shapes=[
             pltpu.VMEM((rows // LANES, LANES), jnp.int32),
             pltpu.VMEM((rows, width), BF16),
@@ -474,18 +502,17 @@
             pltpu.VMEM((rows, ranks), BF16),
             pltpu.VMEM((rows, ranks), F32),
             pltpu.VMEM((rows, ranks), F32),
+            pltpu.VMEM((rows, ranks), F32),
             pltpu.VMEM((rows, ranks), BF16),
             pltpu.VMEM((rows, 2 * ranks), BF16),
             pltpu.VMEM((ranks, rows), BF16),
             pltpu.VMEM((ranks, rows), BF16),
             pltpu.VMEM((2 * experts, rows), BF16),
             pltpu.VMEM((every, LANES), F32),
-            pltpu.VMEM((every, LANES), F32),
             pltpu.VMEM((every // 2, LANES), F32),
             pltpu.VMEM((3, every // 8, LANES), F32),
             pltpu.VMEM((3, every // 32, LANES), F32),
             pltpu.VMEM((4, every // 32, LANES), F32),
-            pltpu.VMEM((4, 8, LANES), F32),
             pltpu.VMEM((8, 8, LANES), F32),
             pltpu.VMEM((2, SIDE, 8, LANES), F32),
             pltpu.SemaphoreType.DMA((6,)),
@@ -496,12 +523,33 @@
             pltpu.SemaphoreType.DMA((3, 7)),
         ],
         compiler_params=pltpu.CompilerParams(
-            collective_id=0, has_side_effects=True, vmem_limit_bytes=48 * 1024 * 1024
+            collective_id=0, has_side_effects=True, vmem_limit_bytes=46 * 1024 * 1024
         ),
         name="step",
     )(token_ids.reshape(rows // LANES, LANES), tokens, frozen_weight, adapter_down, adapter_up, gate_weight.T, upstream)
-    projected, input_grad, down, up, gate, stats = found
-    return projected, input_grad, down, up, gate.T, stats[0, :experts], stats[1, 0]
+    projected, input_grad, down, up, gate, load, entropy = pl.pallas_call(
+        functools.partial(finish_kernel, (width, outputs, ranks, experts)),
+        out_shape=(
+            jax.ShapeDtypeStruct((rows, outputs), BF16),
+            jax.ShapeDtypeStruct((rows, width), BF16),
+            jax.ShapeDtypeStruct((width, ranks), F32),
+            jax.ShapeDtypeStruct((ranks, outputs), F32),
+            jax.ShapeDtypeStruct((experts, width), F32),
+            jax.ShapeDtypeStruct((experts,), F32),
+            jax.ShapeDtypeStruct((1,), F32),
+        ),
+        in_specs=[vmem] * 4,
+        out_specs=(anywhere,) * 5 + (smem,) * 2,
+        scratch_shapes=[
+            pltpu.VMEM((width, ranks), F32),
+            pltpu.VMEM((ranks, outputs), F32),
+            pltpu.VMEM((experts, width), F32),
+            pltpu.SemaphoreType.DMA((8,)),
+        ],
+        compiler_params=pltpu.CompilerParams(vmem_limit_bytes=20 * 1024 * 1024),
+        name="finish",
+    )(*held)
+    return projected, input_grad, down, up, gate.T, load, entropy.reshape(())
 
 
 def solution(mesh):

time: 68.5 us -> 62.6 us (0.914)
  local copies, waits for them, and re-layouts: 8.51 us -> 0 us
  Pallas kernels: 59.3 us -> 61.7 us
    unnamed x5 -> x0, local copies, waits for them, and re-layouts: 7.48 us -> none
    pallas_call x0 -> x1, Pallas kernels: none -> 5.43 us  [on_device(): pl.pallas_call(functools.partial(finish_kernel, (width, outputs, ranks, e...]
    pallas_call x1, Pallas kernels: 59.3 us -> 56.2 us  [on_device(): pl.pallas_call(functools.partial(kernel, (rows, width, outputs, ranks, ex...]
where the time goes in v3:
time: 62.6 us; the launch traced here: 62.5 us
  Pallas kernels  61.7 us (99%)
  between operations  0.8 us (1%)
    pallas_call x1, Pallas kernels, on_device(): pl.pallas_call(functools.partial(kernel, (rows, width, outputs, ranks, ex...  56.2 us
    pallas_call x1, Pallas kernels, on_device(): pl.pallas_call(functools.partial(finish_kernel, (width, outputs, ranks, e...  5.43 us

profile of v3, /device:TPU:1, one launch (start us, length us, event | category | flops | bytes accessed | tf_op | source)
XLA Modules:
  0.0 62.5 jit_solution(5859496208350526728)
XLA Ops:
  0.6 56.2 %step.1 = (bf16[1024,1024]{1,0:T(8,128)(2,1)S(1)}, bf16[1024,4096]{1,0:T(8,128)(2,1)S(1)}, f32[5376,128]{1,0:T(8,128)S(1)}, f32[4,8,128]{2,1,0:T(8,128)S(1)}) custom-call(s32[8,128]{1,0:T(8,128)} %bitcast.5, bf16[1024,4096]{1,0:T(8,128)(2,1)} %tokens_hbm.1, bf16[4096,1024]{1,0:T(8,128)(2,1)} %frozen_hbm.1, bf16[4096,128]{1,0:T(8,128)(2,1)} %down_hbm.1, ...), custom_call_target="tpu_custom_call" | custom-call | tf_op jit(solution)/shard_map/step/pallas_call | solution.py:484
  56.9 5.4 %finish.1 = (bf16[1024,1024]{1,0:T(8,128)(2,1)}, bf16[1024,4096]{1,0:T(8,128)(2,1)}, f32[4096,128]{1,0:T(8,128)}, f32[128,1024]{1,0:T(8,128)}, f32[8,4096]{1,0:T(8,128)}, /*index=5*/f32[8]{0:T(128)}, f32[1]{0:T(128)}) custom-call(bf16[1024,1024]{1,0:T(8,128)(2,1)S(1)} %get-tuple-element.18.projected, bf16[1024,4096]{1,0:T(8,128)(2,1)S(1)} %get-tuple-element.19.inputs, ...), custom_call_target="tpu_custom_call" | custom-call | tf_op jit(solution)/shard_map/finish/pallas_call | solution.py:530

commit v4 on v3

--- a/solution.py
+++ b/solution.py
@@ -59,28 +59,41 @@
     def last_at(self, piece, place, second):
         return self.quarter_at(piece, place) + second * piece.last
 
-    def copies(self, phase, piece):
+    def send_to(self, source, target, phase, piece, device):
+        pltpu.make_async_remote_copy(
+            src_ref=source,
+            dst_ref=target,
+            send_sem=self.send.at[piece.index],
+            recv_sem=self.recv.at[phase, piece.index],
+            device_id=device,
+            device_id_type=MESH,
+        ).start()
+
+    def sent(self, piece, rows):
+        here = self.part.at[pl.ds(0, rows)]
+        pltpu.make_async_copy(here, here, self.send.at[piece.index]).wait()
+
+    def received(self, phase, piece, rows):
+        here = self.part.at[pl.ds(0, rows)]
+        pltpu.make_async_copy(here, here, self.recv.at[phase, piece.index]).wait()
+
+    def forward(self, piece, distance):
+        place = lax.rem(lax.axis_index(piece.first) + distance, SIDE)
+        here = self.total.at[span(self.quarter_at(piece, place), piece.quarter)]
+        self.send_to(here, here, 6, piece, {CORE: 1 - self.core})
+
+    def start(self, phase, piece):
         one, two = lax.axis_index(piece.first), lax.axis_index(piece.second)
-
-        def copy(source, target, slot, device):
-            return pltpu.make_async_remote_copy(
-                src_ref=source,
-                dst_ref=target,
-                send_sem=self.send.at[phase, piece.index, slot],
-                recv_sem=self.recv.at[phase, piece.index, slot],
-                device_id=device,
-                device_id_type=MESH,
-            )
-
         if phase == 0:
             source = self.part.at[span(self.half_at(piece, 1 - self.core), piece.half)]
             target = self.halves.at[pl.ds(piece.base // 2, piece.half)]
-            return [copy(source, target, 0, {CORE: 1 - self.core})]
+            self.send_to(source, target, 0, piece, {CORE: 1 - self.core})
+            return
         if phase == 6:
-            here = self.total.at[span(self.half_at(piece, self.core), piece.half)]
-            return [copy(here, here, 0, {CORE: 1 - self.core})]
-        made = []
-        for distance in (1, 2, 3):
+            for distance in (1, 2, 3):
+                self.forward(piece, distance)
+            return
+        for distance in (2, 1, 3):
             slot = distance - 1
             if phase == 1:
                 place = lax.rem(one + distance, SIDE)
@@ -102,16 +115,15 @@
             else:
                 source = self.total.at[span(self.quarter_at(piece, one), piece.quarter)]
                 target, axis = source, piece.first
-            made.append(copy(source, target, slot, ring_peer(axis, distance)))
-        return made
-
-    def start(self, phase, piece):
-        for copy in self.copies(phase, piece):
-            copy.start()
+            self.send_to(source, target, phase, piece, ring_peer(axis, distance))
+        if phase == 5:
+            self.forward(piece, 0)
 
     def finish(self, phase, piece):
-        for copy in self.copies(phase, piece):
-            copy.wait()
+        sent = {0: piece.half, 1: 3 * piece.quarter, 5: 4 * piece.quarter, 6: 3 * piece.quarter}
+        got_rows = {0: piece.half, 1: 3 * piece.quarter, 5: 3 * piece.quarter, 6: piece.half}
+        self.sent(piece, sent.get(phase, 3 * piece.last))
+        self.received(phase, piece, got_rows.get(phase, 3 * piece.last))
         one, two = lax.axis_index(piece.first), lax.axis_index(piece.second)
         if phase == 0:
             here = span(self.half_at(piece, self.core), piece.half)
@@ -143,8 +155,7 @@
         self.tiles, self.wide, self.narrow = tiles, wide, narrow
         self.send, self.recv = send, recv
 
-    def copies(self, stage):
-        made = []
+    def start(self, stage):
         for distance in range(1, 8 if stage == 0 else SIDE):
             if stage == 0:
                 mine = lax.axis_index(CORE) * SIDE + lax.axis_index(AXES[0])
@@ -154,25 +165,19 @@
             else:
                 device = ring_peer(AXES[stage], distance)
                 target = self.narrow.at[stage - 1, lax.axis_index(AXES[stage])]
-            made.append(
-                pltpu.make_async_remote_copy(
-                    src_ref=self.tiles.at[stage],
-                    dst_ref=target,
-                    send_sem=self.send.at[stage, distance - 1],
-                    recv_sem=self.recv.at[stage, distance - 1],
-                    device_id=device,
-                    device_id_type=MESH,
-                )
-            )
-        return made
-
-    def start(self, stage):
-        for copy in self.copies(stage):
-            copy.start()
+            pltpu.make_async_remote_copy(
+                src_ref=self.tiles.at[stage],
+                dst_ref=target,
+                send_sem=self.send.at[0],
+                recv_sem=self.recv.at[stage],
+                device_id=device,
+                device_id_type=MESH,
+            ).start()
 
     def finish(self, stage):
-        for copy in self.copies(stage):
-            copy.wait()
+        several = self.wide.at[pl.ds(0, 7 if stage == 0 else 3)]
+        pltpu.make_async_copy(several, several, self.send.at[0]).wait()
+        pltpu.make_async_copy(several, several, self.recv.at[stage]).wait()
         if stage == 0:
             self.wide[lax.axis_index(CORE) * SIDE + lax.axis_index(AXES[0])] = self.tiles[0]
             got = [self.wide[place] for place in range(8)]
@@ -185,23 +190,85 @@
         self.tiles[stage + 1] = total
 
 
+class GateExchange:
+    def __init__(self, base, rows, part, total, inward, plane, send, recv):
+        self.base, self.share = base, rows // 8
+        self.part, self.total = part, total
+        self.inward, self.plane = inward, plane
+        self.send, self.recv = send, recv
+        self.group = lax.axis_index(CORE) * SIDE + lax.axis_index(AXES[0])
+        self.spot = lax.axis_index(AXES[1]) * SIDE + lax.axis_index(AXES[2])
+
+    def chunk(self, place):
+        return span(self.base + place * self.share, self.share)
+
+    def start(self, stage):
+        mine = self.chunk(self.group)
+        for distance in range(1, 16 if stage == 1 else 8):
+            if stage == 1:
+                other = lax.rem(self.spot + distance, 16)
+                device = {AXES[1]: lax.div(other, SIDE), AXES[2]: lax.rem(other, SIDE)}
+                source, target = self.part.at[mine], self.plane.at[self.spot]
+            else:
+                other = lax.rem(self.group + distance, 8)
+                device = {CORE: lax.div(other, SIDE), AXES[0]: lax.rem(other, SIDE)}
+                if stage == 0:
+                    source, target = self.part.at[self.chunk(other)], self.inward.at[distance - 1]
+                else:
+                    source = self.total.at[mine]
+                    target = source
+            pltpu.make_async_remote_copy(
+                src_ref=source,
+                dst_ref=target,
+                send_sem=self.send.at[3],
+                recv_sem=self.recv.at[stage],
+                device_id=device,
+                device_id_type=MESH,
+            ).start()
+
+    def finish(self, stage):
+        several = self.plane.at[pl.ds(0, 15 if stage == 1 else 7)]
+        pltpu.make_async_copy(several, several, self.send.at[3]).wait()
+        pltpu.make_async_copy(several, several, self.recv.at[stage]).wait()
+        mine = self.chunk(self.group)
+        if stage == 0:
+            value = self.part[mine]
+            for slot in range(7):
+                value = value + self.inward[slot]
+            self.part[mine] = value
+        elif stage == 1:
+            self.plane[self.spot] = self.part[mine]
+            value = self.plane[0]
+            for slot in range(1, 16):
+                value = value + self.plane[slot]
+            self.total[mine] = value
+
+    def step(self, stage):
+        self.finish(stage)
+        self.start(stage + 1)
+
+
 def peers():
     core, x = lax.axis_index(CORE), lax.axis_index(AXES[0])
+    spot = lax.axis_index(AXES[1]) * SIDE + lax.axis_index(AXES[2])
     found = [{CORE: 1 - core}]
     for distance in (1, 2, 3):
         found.append({CORE: 1 - core, AXES[0]: lax.rem(x + distance, SIDE)})
-        found += [ring_peer(axis, distance) for axis in AXES]
+        found.append(ring_peer(AXES[0], distance))
+    for distance in range(1, 16):
+        other = lax.rem(spot + distance, 16)
+        found.append({AXES[1]: lax.div(other, SIDE), AXES[2]: lax.rem(other, SIDE)})
     return found
 
 
 def kernel(
     sizes,
     ids_hbm, tokens_hbm, frozen_hbm, down_hbm, up_hbm, gate_hbm, upstream_hbm,
-    projected_ref, input_ref, total, tiles,
-    ids, tokens, frozen, sides, up, gate, masked,
-    low, prob, plain, turned, weighted, grads, grads_t, weighted_t, gate_t,
-    part, halves, firsts, seconds, thirds, wide, narrow,
-    load_sem, token_sem, send, recv, stat_send, stat_recv,
+    projected_ref, input_ref, total, tiles, frozen, sides, masked, grads,
+    ids, tokens, up, gate,
+    both, low, prob, plain, turned, weighted, grads_t, weighted_t, gate_t,
+    part, halves, firsts, seconds, thirds, wide, narrow, inward, plane,
+    load_sem, token_sem, send, recv, stat_send, stat_recv, gate_recv,
 ):
     rows, width, outputs, ranks, experts = sizes
     rank = ranks // experts
@@ -209,10 +276,15 @@
     chunks = rows // CHUNK
     up_base = width
     gate_base = width + outputs
-    pieces = (Piece(0, 0, 1792), Piece(1, 1792, 1792), Piece(2, 3584, gate_base - 3584), Piece(3, gate_base, width * experts // LANES))
+    pieces = (Piece(0, 0, 1792), Piece(1, 1792, 1792), Piece(2, 3584, gate_base - 3584))
     exchange = Exchange(part, total, halves, firsts, seconds, thirds, send, recv)
     statistics = Statistics(tiles, wide, narrow, stat_send, stat_recv)
-
+    gates = GateExchange(gate_base, width * experts // LANES, part, total, inward, plane, send, gate_recv)
+
+    gate_load = pltpu.make_async_copy(gate_hbm, gate, load_sem.at[0])
+    ids_load = pltpu.make_async_copy(ids_hbm, ids, load_sem.at[1])
+    gate_load.start()
+    ids_load.start()
     barrier = pltpu.get_barrier_semaphore()
     greeted = peers()
     for peer in greeted:
@@ -225,19 +297,15 @@
         here = span(chunk * CHUNK, CHUNK, CHUNK)
         return pltpu.make_async_copy(tokens_hbm.at[here], tokens.at[here], token_sem.at[chunk])
 
-    gate_load = load(gate_hbm, gate, 0)
-    ids_load = load(ids_hbm, ids, 1)
     down_load = load(down_hbm, sides.at[:, pl.ds(0, ranks)], 2)
     up_load = load(up_hbm, up, 3)
     upstream_load = load(upstream_hbm, masked, 4)
     frozen_load = load(frozen_hbm, frozen, 5)
-    gate_load.start()
-    ids_load.start()
     down_load.start()
-    for chunk in range(chunks):
-        token_load(chunk).start()
+    token_load(0).start()
 
     gate_load.wait()
+    token_load(1).start()
 
     @pl.loop(0, width // 512)
     def _(block):
@@ -259,23 +327,11 @@
     tiles[0] = jnp.zeros((8, LANES), F32)
     down_load.wait()
 
-    @pl.loop(0, chunks)
-    def _(chunk):
+    def shares(chunk):
         here = span(chunk * CHUNK, CHUNK, CHUNK)
-        token_load(chunk).wait()
-
-        @pl.when(chunk == 1)
-        def _():
-            up_load.start()
-            upstream_load.start()
-
-        @pl.when(chunk == 3)
-        def _():
-            frozen_load.start()
-
-        both = dot(tokens[here], sides[...])
-        low[here] = both[:, :ranks].astype(BF16)
-        logits = both[:, ranks:]
+        slot = chunk % 2
+        low[here] = both[slot, :, :ranks].astype(BF16)
+        logits = both[slot, :, ranks:]
         shifted = logits - jnp.max(logits, axis=1, keepdims=True)
         raised = jnp.exp(shifted)
         mass = lane_sum(raised) * scale
@@ -289,6 +345,21 @@
         tiles[0, 1:2] += jnp.sum(alive * entropy, axis=0, keepdims=True)
         tiles[0, 2:3] += jnp.sum(alive, axis=0, keepdims=True)
 
+    token_load(2).start()
+    token_load(0).wait()
+    token_load(3).start()
+    both[0] = dot(tokens[0:CHUNK], sides[...])
+    up_load.start()
+    upstream_load.start()
+
+    @pl.loop(1, chunks)
+    def _(chunk):
+        token_load(chunk).wait()
+        shares(chunk - 1)
+        both[chunk % 2] = dot(tokens[span(chunk * CHUNK, CHUNK, CHUNK)], sides[...])
+
+    frozen_load.start()
+    shares(chunks - 1)
     pl.semaphore_wait(barrier, len(greeted))
     statistics.start(0)
 
@@ -318,6 +389,8 @@
     down_block(0, 896)
     down_block(896, 896)
     exchange.start(0, pieces[0])
+    statistics.finish(0)
+    statistics.start(1)
     down_block(1792, 896)
     down_block(2688, 896)
     exchange.start(0, pieces[1])
@@ -326,15 +399,14 @@
     for block in range(outputs // LANES):
         part[up_base + block * LANES : up_base + (block + 1) * LANES] = found[:, block * LANES : (block + 1) * LANES]
     exchange.start(0, pieces[2])
+    statistics.finish(1)
+    statistics.start(2)
     exchange.step(0, pieces[0])
-    statistics.finish(0)
-    statistics.start(1)
     group = lax.broadcasted_iota(jnp.int32, (2 * ranks, ranks), 0) % ranks // rank
     member = lax.broadcasted_iota(jnp.int32, (2 * ranks, ranks), 1) // rank
     blocks = (group == member).astype(F32).astype(BF16)
 
-    @pl.loop(0, chunks)
-    def _(chunk):
+    def task_part(chunk):
         here = span(chunk * CHUNK, CHUNK, CHUNK)
         share = prob[here]
         product = low[here].astype(F32) * turned[here]
@@ -344,43 +416,15 @@
         plain[here] += share * (task - lane_sum(share * task) * scale)
 
     exchange.step(0, pieces[1])
-
-    def base_blocks(first, last):
-        @pl.loop(first, last)
-        def _(block):
-            tall = span((block % 2) * (rows // 2), rows // 2, rows // 2)
-            here = span((block // 2) * 256, 256, 256)
-            found = dot(tokens[tall], frozen[:, here]) + dot(weighted[tall], up[:, here])
-            projected_ref[tall, here] = found.astype(BF16)
-
-    def input_blocks(first, last):
-        @pl.loop(first, last)
-        def _(block):
-            here = span(block * 512, 512, 512)
-            found = right_dot(masked[...], frozen[here]) + right_dot(grads[...], sides[here])
-            input_ref[:, here] = found.astype(BF16)
-
-    def step_all(phase):
-        for piece in pieces[:3]:
-            exchange.step(phase, piece)
-
-    frozen_load.wait()
-    base_blocks(0, 1)
-    exchange.step(0, pieces[2])
-    statistics.finish(1)
-    statistics.start(2)
-    base_blocks(1, 3)
-    statistics.finish(2)
-    load_all, live_all = tiles[3, 0:1], tiles[3, 2:3]
-    push = (2.0 * experts * 100.0) / live_all
     lane = lax.broadcasted_iota(jnp.int32, (CHUNK, LANES), 1)
     pick_from = lax.broadcasted_iota(jnp.int32, (ranks, ranks), 0)
     pick_to = lax.broadcasted_iota(jnp.int32, (ranks, ranks), 1)
     pick = (pick_from == (pick_to % experts) * rank + pick_to // experts).astype(F32)
     pick = jnp.where(pick_to < 2 * experts, pick, 0.0).astype(BF16)
 
-    @pl.loop(0, chunks)
-    def _(chunk):
+    def slope_part(chunk):
+        load_all, live_all = tiles[3, 0:1], tiles[3, 2:3]
+        push = (2.0 * experts * 100.0) / live_all
         here = span(chunk * CHUNK, CHUNK, CHUNK)
         share = prob[here]
         slope = share * (load_all - lane_sum(share * load_all) * scale)
@@ -391,6 +435,33 @@
         grads[here, ranks : 2 * ranks] = packed
         gate_t[:, here] = dot(packed, pick).T[: 2 * experts].astype(BF16)
 
+    def base_block(block):
+        tall = span((block % 2) * (rows // 2), rows // 2, rows // 2)
+        here = span((block // 2) * 256, 256, 256)
+        found = dot(tokens[tall], frozen[:, here]) + dot(weighted[tall], up[:, here])
+        projected_ref[tall, here] = found.astype(BF16)
+
+    def step_all(phase):
+        for piece in pieces[:3]:
+            exchange.step(phase, piece)
+
+    frozen_load.wait()
+    exchange.step(0, pieces[2])
+
+    @pl.loop(0, 2)
+    def _(block):
+        task_part(2 * block)
+        task_part(2 * block + 1)
+        base_block(block)
+
+    statistics.finish(2)
+
+    @pl.loop(2, 4)
+    def _(block):
+        slope_part(2 * block - 4)
+        slope_part(2 * block - 3)
+        base_block(block)
+
     @pl.loop(0, width // 1024)
     def _(block):
         found = dot(gate_t[...], tokens[:, span(block * 1024, 1024, 1024)])
@@ -399,41 +470,65 @@
             here = span(gate_base + (block * 8 + piece) * experts, experts)
             part[here] = found[:, piece * LANES : (piece + 1) * LANES]
 
-    exchange.start(0, pieces[3])
-    base_blocks(3, 4)
-    exchange.step(0, pieces[3])
-    step_all(1)
-    base_blocks(4, 7)
-    exchange.step(1, pieces[3])
-    step_all(2)
-    base_blocks(7, 8)
-    input_blocks(0, 1)
-    exchange.step(2, pieces[3])
-    step_all(3)
-    input_blocks(1, 3)
-    exchange.step(3, pieces[3])
-    step_all(4)
-    input_blocks(3, 5)
-    exchange.step(4, pieces[3])
-    input_blocks(5, 8)
-    step_all(5)
-    exchange.step(5, pieces[3])
+    gates.start(0)
+
+    @pl.loop(4, 8)
+    def _(block):
+        @pl.when(block == 4)
+        def _():
+            exchange.step(1, pieces[0])
+
+        @pl.when(block == 5)
+        def _():
+            exchange.step(1, pieces[1])
+            exchange.step(1, pieces[2])
+
+        @pl.when(block == 7)
+        def _():
+            step_all(2)
+            gates.step(0)
+
+        base_block(block)
+
+    @pl.loop(0, input_ref.shape[1] // 512)
+    def _(block):
+        @pl.when(block == 1)
+        def _():
+            step_all(3)
+
+        @pl.when(block == 2)
+        def _():
+            gates.step(1)
+
+        @pl.when(block == 3)
+        def _():
+            step_all(4)
+
+        @pl.when(block == 5)
+        def _():
+            step_all(5)
+
+        here = span(block * 512, 512, 512)
+        found = right_dot(masked[...], frozen[here]) + right_dot(grads[...], sides[here])
+        input_ref[:, here] = found.astype(BF16)
+
+    gates.finish(2)
     for piece in pieces:
         exchange.finish(6, piece)
 
 
 def finish_kernel(
     sizes,
-    projected, inputs, total, tiles,
+    projected, inputs, total, tiles, frozen, sides, masked, grads,
     projected_hbm, input_hbm, down_hbm, up_hbm, gate_hbm, load_ref, entropy_ref,
-    scaled, up, gate, sems,
+    scaled, up, gate, rest, sems,
 ):
     width, outputs, ranks, experts = sizes
     rank = ranks // experts
     every = total.shape[0]
     quarter = width // 4
     copies = [
-        pltpu.make_async_copy(inputs, input_hbm, sems.at[0]),
+        pltpu.make_async_copy(inputs, input_hbm.at[:, pl.ds(0, inputs.shape[1])], sems.at[0]),
         pltpu.make_async_copy(projected, projected_hbm, sems.at[1]),
     ]
     for copy in copies:
@@ -464,6 +559,13 @@
     copy = pltpu.make_async_copy(gate, gate_hbm, sems.at[7])
     copy.start()
     copies.append(copy)
+    for block in range(2):
+        here = pl.ds(inputs.shape[1] + block * 512, 512)
+        found = right_dot(masked[...], frozen[here]) + right_dot(grads[...], sides[here])
+        rest[block] = found.astype(BF16)
+        copy = pltpu.make_async_copy(rest.at[block], input_hbm.at[:, here], sems.at[8 + block])
+        copy.start()
+        copies.append(copy)
     mean = tiles[3] / tiles[3, 2:3]
     lane = lax.broadcasted_iota(jnp.int32, (1, LANES), 1)
     for expert in range(experts):
@@ -479,32 +581,34 @@
     experts = gate_weight.shape[1]
     every = width + outputs + width * experts // LANES
     anywhere = pl.BlockSpec(memory_space=pl.ANY)
+    hbm = pl.BlockSpec(memory_space=pltpu.HBM)
     vmem = pl.BlockSpec(memory_space=pltpu.VMEM)
     smem = pl.BlockSpec(memory_space=pltpu.SMEM)
     held = pl.pallas_call(
         functools.partial(kernel, (rows, width, outputs, ranks, experts)),
         out_shape=(
             pltpu.VMEM((rows, outputs), BF16),
-            pltpu.VMEM((rows, width), BF16),
+            pltpu.VMEM((rows, width - 1024), BF16),
             pltpu.VMEM((every, LANES), F32),
             pltpu.VMEM((4, 8, LANES), F32),
+            pltpu.VMEM((width, outputs), BF16),
+            pltpu.VMEM((width, 2 * ranks), BF16),
+            pltpu.VMEM((rows, outputs), BF16),
+            pltpu.VMEM((rows, 2 * ranks), BF16),
         ),
-        in_specs=[anywhere] * 7,
-        out_specs=(vmem,) * 4,
+        in_specs=[hbm] * 7,
+        out_specs=(vmem,) * 8,
         scratch_shapes=[
             pltpu.VMEM((rows // LANES, LANES), jnp.int32),
             pltpu.VMEM((rows, width), BF16),
-            pltpu.VMEM((width, outputs), BF16),
-            pltpu.VMEM((width, 2 * ranks), BF16),
             pltpu.VMEM((ranks, outputs), BF16),
             pltpu.VMEM((experts, width), BF16),
-            pltpu.VMEM((rows, outputs), BF16),
+            pltpu.VMEM((2, CHUNK, 2 * ranks), F32),
             pltpu.VMEM((rows, ranks), BF16),
             pltpu.VMEM((rows, ranks), F32),
             pltpu.VMEM((rows, ranks), F32),
             pltpu.VMEM((rows, ranks), F32),
             pltpu.VMEM((rows, ranks), BF16),
-            pltpu.VMEM((rows, 2 * ranks), BF16),
             pltpu.VMEM((ranks, rows), BF16),
             pltpu.VMEM((ranks, rows), BF16),
             pltpu.VMEM((2 * experts, rows), BF16),
@@ -515,15 +619,18 @@
             pltpu.VMEM((4, every // 32, LANES), F32),
             pltpu.VMEM((8, 8, LANES), F32),
             pltpu.VMEM((2, SIDE, 8, LANES), F32),
+            pltpu.VMEM((7, width * experts // LANES // 8, LANES), F32),
+            pltpu.VMEM((16, width * experts // LANES // 8, LANES), F32),
             pltpu.SemaphoreType.DMA((6,)),
             pltpu.SemaphoreType.DMA((rows // CHUNK,)),
-            pltpu.SemaphoreType.DMA((7, 4, 3)),
-            pltpu.SemaphoreType.DMA((7, 4, 3)),
-            pltpu.SemaphoreType.DMA((3, 7)),
-            pltpu.SemaphoreType.DMA((3, 7)),
+            pltpu.SemaphoreType.DMA((4,)),
+            pltpu.SemaphoreType.DMA((7, 3)),
+            pltpu.SemaphoreType.DMA((1,)),
+            pltpu.SemaphoreType.DMA((3,)),
+            pltpu.SemaphoreType.DMA((3,)),
         ],
         compiler_params=pltpu.CompilerParams(
-            collective_id=0, has_side_effects=True, vmem_limit_bytes=46 * 1024 * 1024
+            collective_id=0, has_side_effects=True, vmem_limit_bytes=34 * 1024 * 1024
         ),
         name="step",
     )(token_ids.reshape(rows // LANES, LANES), tokens, frozen_weight, adapter_down, adapter_up, gate_weight.T, upstream)
@@ -538,15 +645,16 @@
             jax.ShapeDtypeStruct((experts,), F32),
             jax.ShapeDtypeStruct((1,), F32),
         ),
-        in_specs=[vmem] * 4,
+        in_specs=[vmem] * 8,
         out_specs=(anywhere,) * 5 + (smem,) * 2,
         scratch_shapes=[
             pltpu.VMEM((width, ranks), F32),
             pltpu.VMEM((ranks, outputs), F32),
             pltpu.VMEM((experts, width), F32),
-            pltpu.SemaphoreType.DMA((8,)),
+            pltpu.VMEM((2, rows, 512), BF16),
+            pltpu.SemaphoreType.DMA((10,)),
         ],
-        compiler_params=pltpu.CompilerParams(vmem_limit_bytes=20 * 1024 * 1024),
+        compiler_params=pltpu.CompilerParams(vmem_limit_bytes=16 * 1024 * 1024),
         name="finish",
     )(*held)
     return projected, input_grad, down, up, gate.T, load, entropy.reshape(())

time: 62.6 us -> 54.8 us (0.88)
  Pallas kernels: 61.7 us -> 54.1 us
    pallas_call x1, Pallas kernels: 56.2 us -> 48.4 us  [on_device(): pl.pallas_call(functools.partial(kernel, (rows, width, outputs, ranks, ex...]
where the time goes in v4:
time: 54.8 us; the launch traced here: 54.7 us
  Pallas kernels  54.1 us (99%)
  between operations  0.64 us (1%)
    pallas_call x1, Pallas kernels, on_device(): pl.pallas_call(functools.partial(kernel, (rows, width, outputs, ranks, ex...  48.4 us
    pallas_call x1, Pallas kernels, on_device(): pl.pallas_call(functools.partial(finish_kernel, (width, outputs, ranks, e...  5.69 us

profile of v4, /device:TPU:1, one launch (start us, length us, event | category | flops | bytes accessed | tf_op | source)
XLA Modules:
  0.0 54.7 jit_solution(7869365295679243940)
XLA Ops:
  0.6 48.4 %step.1 = (bf16[1024,1024]{1,0:T(8,128)(2,1)S(1)}, bf16[1024,3072]{1,0:T(8,128)(2,1)S(1)}, f32[5376,128]{1,0:T(8,128)S(1)}, f32[4,8,128]{2,1,0:T(8,128)S(1)}, bf...) custom-call(s32[8,128]{1,0:T(8,128)} %bitcast.5, ...), custom_call_target="tpu_custom_call" | custom-call | tf_op jit(solution)/shard_map/step/pallas_call | solution.py:587
  49.0 5.7 %finish.1 = (bf16[1024,1024]{1,0:T(8,128)(2,1)}, bf16[1024,4096]{1,0:T(8,128)(2,1)}, f32[4096,128]{1,0:T(8,128)}, f32[128,1024]{1,0:T(8,128)}, f32[8,4096]{1,0:T(8,128)}, /*index=5*/f32[8]{0:T(128)}, f32[1]{0:T(128)}) custom-call(bf16[1024,1024]{1,0:T(8,128)(2,1)S(1)} %get-tuple-element.22.projected, bf16[1024,3072]{1,0:T(8,128)(2,1)S(1)} %get-tuple-element.23.inputs, ...), custom_call_target="tpu_custom_call" | custom-call | tf_op jit(solution)/shard_map/finish/pallas_call | solution.py:637

commit v5 on v4

--- a/solution.py
+++ b/solution.py
@@ -82,6 +82,12 @@
         here = self.total.at[span(self.quarter_at(piece, place), piece.quarter)]
         self.send_to(here, here, 6, piece, {CORE: 1 - self.core})
 
+    def spread_out(self, piece, place):
+        here = self.total.at[span(self.last_at(piece, lax.axis_index(piece.first), place), piece.last)]
+        for distance in (2, 1, 3):
+            self.send_to(here, here, 5, piece, ring_peer(piece.first, distance))
+        self.send_to(here, here, 6, piece, {CORE: 1 - self.core})
+
     def start(self, phase, piece):
         one, two = lax.axis_index(piece.first), lax.axis_index(piece.second)
         if phase == 0:
@@ -89,18 +95,30 @@
             target = self.halves.at[pl.ds(piece.base // 2, piece.half)]
             self.send_to(source, target, 0, piece, {CORE: 1 - self.core})
             return
+        if phase == 1:
+            for turn in (1, 2, 3, 0):
+                second = lax.rem(two + turn, SIDE)
+                for distance in (2, 1, 3):
+                    place = lax.rem(one + distance, SIDE)
+                    self.send_to(
+                        self.part.at[span(self.last_at(piece, place, second), piece.last)],
+                        self.firsts.at[distance - 1, span(piece.base // 8 + second * piece.last, piece.last)],
+                        7 if turn == 0 else 1,
+                        piece,
+                        ring_peer(piece.first, distance),
+                    )
+            return
+        if phase == 5:
+            for distance in (1, 2, 3):
+                self.spread_out(piece, lax.rem(two + distance, SIDE))
+            return
         if phase == 6:
             for distance in (1, 2, 3):
                 self.forward(piece, distance)
             return
         for distance in (2, 1, 3):
             slot = distance - 1
-            if phase == 1:
-                place = lax.rem(one + distance, SIDE)
-                source = self.part.at[span(self.quarter_at(piece, place), piece.quarter)]
-                target = self.firsts.at[slot, pl.ds(piece.base // 8, piece.quarter)]
-                axis = piece.first
-            elif phase == 2:
+            if phase == 2:
                 place = lax.rem(two + distance, SIDE)
                 source = self.part.at[span(self.last_at(piece, one, place), piece.last)]
                 target = self.seconds.at[slot, pl.ds(piece.base // 32, piece.last)]
@@ -109,19 +127,16 @@
                 source = self.part.at[span(self.last_at(piece, one, two), piece.last)]
                 target = self.thirds.at[lax.axis_index(piece.third), pl.ds(piece.base // 32, piece.last)]
                 axis = piece.third
-            elif phase == 4:
+            else:
                 source = self.total.at[span(self.last_at(piece, one, two), piece.last)]
                 target, axis = source, piece.second
-            else:
-                source = self.total.at[span(self.quarter_at(piece, one), piece.quarter)]
-                target, axis = source, piece.first
             self.send_to(source, target, phase, piece, ring_peer(axis, distance))
-        if phase == 5:
-            self.forward(piece, 0)
+        if phase == 4:
+            self.spread_out(piece, two)
 
     def finish(self, phase, piece):
-        sent = {0: piece.half, 1: 3 * piece.quarter, 5: 4 * piece.quarter, 6: 3 * piece.quarter}
-        got_rows = {0: piece.half, 1: 3 * piece.quarter, 5: 3 * piece.quarter, 6: piece.half}
+        sent = {0: piece.half, 1: 12 * piece.last, 4: 7 * piece.last, 5: 12 * piece.last, 6: 3 * piece.quarter}
+        got_rows = {0: piece.half, 1: 9 * piece.last, 5: 3 * piece.quarter, 6: piece.half}
         self.sent(piece, sent.get(phase, 3 * piece.last))
         self.received(phase, piece, got_rows.get(phase, 3 * piece.last))
         one, two = lax.axis_index(piece.first), lax.axis_index(piece.second)
@@ -129,11 +144,11 @@
             here = span(self.half_at(piece, self.core), piece.half)
             self.part[here] = self.part[here] + self.halves[pl.ds(piece.base // 2, piece.half)]
         elif phase == 1:
-            here = span(self.quarter_at(piece, one), piece.quarter)
-            there = pl.ds(piece.base // 8, piece.quarter)
-            got = self.firsts
-            self.part[here] = (self.part[here] + got[0, there]) + (got[1, there] + got[2, there])
+            for turn in (1, 2, 3):
+                self.add_firsts(piece, lax.rem(two + turn, SIDE))
         elif phase == 2:
+            self.received(7, piece, 3 * piece.last)
+            self.add_firsts(piece, two)
             here = span(self.last_at(piece, one, two), piece.last)
             there = pl.ds(piece.base // 32, piece.last)
             got = self.seconds
@@ -145,70 +160,73 @@
             got[lax.axis_index(piece.third), there] = self.part[here]
             self.total[here] = (got[0, there] + got[1, there]) + (got[2, there] + got[3, there])
 
+    def add_firsts(self, piece, second):
+        here = span(self.last_at(piece, lax.axis_index(piece.first), second), piece.last)
+        there = span(piece.base // 8 + second * piece.last, piece.last)
+        got = self.firsts
+        self.part[here] = (self.part[here] + got[0, there]) + (got[1, there] + got[2, there])
+
     def step(self, phase, piece):
         self.finish(phase, piece)
         self.start(phase + 1, piece)
 
 
+def pair_peer(first, second, size, distance):
+    other = lax.rem(lax.axis_index(first) * SIDE + lax.axis_index(second) + distance, size)
+    return {first: lax.div(other, SIDE), second: lax.rem(other, SIDE)}
+
+
 class Statistics:
-    def __init__(self, tiles, wide, narrow, send, recv):
-        self.tiles, self.wide, self.narrow = tiles, wide, narrow
+    def __init__(self, tiles, wide, plane, send, recv):
+        self.tiles, self.slots = tiles, (wide, plane)
+        self.axes = ((CORE, AXES[2]), (AXES[0], AXES[1]))
         self.send, self.recv = send, recv
 
+    def mine(self, stage):
+        first, second = self.axes[stage]
+        return lax.axis_index(first) * SIDE + lax.axis_index(second)
+
     def start(self, stage):
-        for distance in range(1, 8 if stage == 0 else SIDE):
-            if stage == 0:
-                mine = lax.axis_index(CORE) * SIDE + lax.axis_index(AXES[0])
-                other = lax.rem(mine + distance, 8)
-                device = {CORE: lax.div(other, SIDE), AXES[0]: lax.rem(other, SIDE)}
-                target = self.wide.at[mine]
-            else:
-                device = ring_peer(AXES[stage], distance)
-                target = self.narrow.at[stage - 1, lax.axis_index(AXES[stage])]
+        size = self.slots[stage].shape[0]
+        for distance in range(1, size):
             pltpu.make_async_remote_copy(
                 src_ref=self.tiles.at[stage],
-                dst_ref=target,
+                dst_ref=self.slots[stage].at[self.mine(stage)],
                 send_sem=self.send.at[0],
                 recv_sem=self.recv.at[stage],
-                device_id=device,
+                device_id=pair_peer(*self.axes[stage], size, distance),
                 device_id_type=MESH,
             ).start()
 
     def finish(self, stage):
-        several = self.wide.at[pl.ds(0, 7 if stage == 0 else 3)]
+        slots = self.slots[stage]
+        several = slots.at[pl.ds(0, slots.shape[0] - 1)]
         pltpu.make_async_copy(several, several, self.send.at[0]).wait()
         pltpu.make_async_copy(several, several, self.recv.at[stage]).wait()
-        if stage == 0:
-            self.wide[lax.axis_index(CORE) * SIDE + lax.axis_index(AXES[0])] = self.tiles[0]
-            got = [self.wide[place] for place in range(8)]
-        else:
-            self.narrow[stage - 1, lax.axis_index(AXES[stage])] = self.tiles[stage]
-            got = [self.narrow[stage - 1, place] for place in range(SIDE)]
-        total = got[0]
-        for other in got[1:]:
-            total = total + other
+        slots[self.mine(stage)] = self.tiles[stage]
+        total = slots[0]
+        for place in range(1, slots.shape[0]):
+            total = total + slots[place]
         self.tiles[stage + 1] = total
 
 
 class GateExchange:
-    def __init__(self, base, rows, part, total, inward, plane, send, recv):
+    def __init__(self, base, rows, part, total, inward, rings, send, recv):
         self.base, self.share = base, rows // 8
         self.part, self.total = part, total
-        self.inward, self.plane = inward, plane
+        self.inward, self.rings = inward, rings
         self.send, self.recv = send, recv
         self.group = lax.axis_index(CORE) * SIDE + lax.axis_index(AXES[0])
-        self.spot = lax.axis_index(AXES[1]) * SIDE + lax.axis_index(AXES[2])
 
     def chunk(self, place):
         return span(self.base + place * self.share, self.share)
 
     def start(self, stage):
         mine = self.chunk(self.group)
-        for distance in range(1, 16 if stage == 1 else 8):
-            if stage == 1:
-                other = lax.rem(self.spot + distance, 16)
-                device = {AXES[1]: lax.div(other, SIDE), AXES[2]: lax.rem(other, SIDE)}
-                source, target = self.part.at[mine], self.plane.at[self.spot]
+        for distance in range(1, SIDE if stage in (1, 2) else 8):
+            if stage in (1, 2):
+                device = ring_peer(AXES[stage], distance)
+                source, target = self.part.at[mine], self.rings.at[stage - 1, lax.axis_index(AXES[stage])]
             else:
                 other = lax.rem(self.group + distance, 8)
                 device = {CORE: lax.div(other, SIDE), AXES[0]: lax.rem(other, SIDE)}
@@ -227,7 +245,7 @@
             ).start()
 
     def finish(self, stage):
-        several = self.plane.at[pl.ds(0, 15 if stage == 1 else 7)]
+        several = self.inward.at[pl.ds(0, 3 if stage in (1, 2) else 7)]
         pltpu.make_async_copy(several, several, self.send.at[3]).wait()
         pltpu.make_async_copy(several, several, self.recv.at[stage]).wait()
         mine = self.chunk(self.group)
@@ -236,12 +254,15 @@
             for slot in range(7):
                 value = value + self.inward[slot]
             self.part[mine] = value
-        elif stage == 1:
-            self.plane[self.spot] = self.part[mine]
-            value = self.plane[0]
-            for slot in range(1, 16):
-                value = value + self.plane[slot]
-            self.total[mine] = value
+        elif stage < 3:
+            self.rings[stage - 1, lax.axis_index(AXES[stage])] = self.part[mine]
+            value = self.rings[stage - 1, 0]
+            for slot in range(1, SIDE):
+                value = value + self.rings[stage - 1, slot]
+            if stage == 1:
+                self.part[mine] = value
+            else:
+                self.total[mine] = value
 
     def step(self, stage):
         self.finish(stage)
@@ -249,15 +270,13 @@
 
 
 def peers():
-    core, x = lax.axis_index(CORE), lax.axis_index(AXES[0])
-    spot = lax.axis_index(AXES[1]) * SIDE + lax.axis_index(AXES[2])
+    core = lax.axis_index(CORE)
     found = [{CORE: 1 - core}]
     for distance in (1, 2, 3):
-        found.append({CORE: 1 - core, AXES[0]: lax.rem(x + distance, SIDE)})
-        found.append(ring_peer(AXES[0], distance))
-    for distance in range(1, 16):
-        other = lax.rem(spot + distance, 16)
-        found.append({AXES[1]: lax.div(other, SIDE), AXES[2]: lax.rem(other, SIDE)})
+        for axis in (AXES[0], AXES[2]):
+            found.append({CORE: 1 - core, **ring_peer(axis, distance)})
+        found.append(ring_peer(AXES[2], distance))
+    found += [pair_peer(AXES[0], AXES[1], 16, distance) for distance in range(1, 16)]
     return found
 
 
@@ -267,7 +286,7 @@
     projected_ref, input_ref, total, tiles, frozen, sides, masked, grads,
     ids, tokens, up, gate,
     both, low, prob, plain, turned, weighted, grads_t, weighted_t, gate_t,
-    part, halves, firsts, seconds, thirds, wide, narrow, inward, plane,
+    part, halves, firsts, seconds, thirds, wide, plane, inward, rings,
     load_sem, token_sem, send, recv, stat_send, stat_recv, gate_recv,
 ):
     rows, width, outputs, ranks, experts = sizes
@@ -278,8 +297,8 @@
     gate_base = width + outputs
     pieces = (Piece(0, 0, 1792), Piece(1, 1792, 1792), Piece(2, 3584, gate_base - 3584))
     exchange = Exchange(part, total, halves, firsts, seconds, thirds, send, recv)
-    statistics = Statistics(tiles, wide, narrow, stat_send, stat_recv)
-    gates = GateExchange(gate_base, width * experts // LANES, part, total, inward, plane, send, gate_recv)
+    statistics = Statistics(tiles, wide, plane, stat_send, stat_recv)
+    gates = GateExchange(gate_base, width * experts // LANES, part, total, inward, rings, send, gate_recv)
 
     gate_load = pltpu.make_async_copy(gate_hbm, gate, load_sem.at[0])
     ids_load = pltpu.make_async_copy(ids_hbm, ids, load_sem.at[1])
@@ -293,19 +312,24 @@
     def load(source, target, slot):
         return pltpu.make_async_copy(source, target, load_sem.at[slot])
 
-    def token_load(chunk):
+    def chunk_load(chunk):
         here = span(chunk * CHUNK, CHUNK, CHUNK)
-        return pltpu.make_async_copy(tokens_hbm.at[here], tokens.at[here], token_sem.at[chunk])
+        return (
+            pltpu.make_async_copy(tokens_hbm.at[here], tokens.at[here], token_sem.at[chunk, 0]),
+            pltpu.make_async_copy(upstream_hbm.at[here], masked.at[here], token_sem.at[chunk, 1]),
+        )
 
     down_load = load(down_hbm, sides.at[:, pl.ds(0, ranks)], 2)
     up_load = load(up_hbm, up, 3)
-    upstream_load = load(upstream_hbm, masked, 4)
-    frozen_load = load(frozen_hbm, frozen, 5)
+    frozen_load = load(frozen_hbm, frozen, 4)
     down_load.start()
-    token_load(0).start()
+    chunk_load(0)[0].start()
+    up_load.start()
+    chunk_load(0)[1].start()
 
     gate_load.wait()
-    token_load(1).start()
+    for copy in chunk_load(1):
+        copy.start()
 
     @pl.loop(0, width // 512)
     def _(block):
@@ -327,10 +351,10 @@
     tiles[0] = jnp.zeros((8, LANES), F32)
     down_load.wait()
 
-    def shares(chunk):
+    def spread(chunk):
         here = span(chunk * CHUNK, CHUNK, CHUNK)
         slot = chunk % 2
-        low[here] = both[slot, :, :ranks].astype(BF16)
+        below = both[slot, :, :ranks].astype(BF16)
         logits = both[slot, :, ranks:]
         shifted = logits - jnp.max(logits, axis=1, keepdims=True)
         raised = jnp.exp(shifted)
@@ -339,42 +363,16 @@
         logp = shifted - jnp.log(mass)
         entropy = -lane_sum(share * logp) * scale
         alive = live_of(chunk)
+        low[here] = below
         prob[here] = share
         plain[here] = 50.0 * alive * share * (logp + entropy)
         tiles[0, 0:1] += jnp.sum(alive * share, axis=0, keepdims=True)
         tiles[0, 1:2] += jnp.sum(alive * entropy, axis=0, keepdims=True)
         tiles[0, 2:3] += jnp.sum(alive, axis=0, keepdims=True)
-
-    token_load(2).start()
-    token_load(0).wait()
-    token_load(3).start()
-    both[0] = dot(tokens[0:CHUNK], sides[...])
-    up_load.start()
-    upstream_load.start()
-
-    @pl.loop(1, chunks)
-    def _(chunk):
-        token_load(chunk).wait()
-        shares(chunk - 1)
-        both[chunk % 2] = dot(tokens[span(chunk * CHUNK, CHUNK, CHUNK)], sides[...])
-
-    frozen_load.start()
-    shares(chunks - 1)
-    pl.semaphore_wait(barrier, len(greeted))
-    statistics.start(0)
-
-    up_load.wait()
-    upstream_load.wait()
-
-    @pl.loop(0, chunks)
-    def _(chunk):
-        here = span(chunk * CHUNK, CHUNK, CHUNK)
-        alive = live_of(chunk)[:, 0:1]
-        mine = jnp.where(alive > 0.0, masked[here].astype(F32), 0.0).astype(BF16)
+        mine = jnp.where(alive[:, 0:1] > 0.0, masked[here].astype(F32), 0.0).astype(BF16)
         masked[here] = mine
         back = right_dot(mine, up[...])
-        share = prob[here]
-        heavy = (low[here].astype(F32) * share).astype(BF16).astype(F32) * 2.0
+        heavy = (below.astype(F32) * share).astype(BF16).astype(F32) * 2.0
         steep = (2.0 * share * back).astype(BF16)
         turned[here] = back
         weighted[here] = heavy.astype(BF16)
@@ -382,6 +380,27 @@
         grads_t[:, here] = steep.astype(F32).T.astype(BF16)
         weighted_t[:, here] = heavy.T.astype(BF16)
 
+    for copy in chunk_load(2):
+        copy.start()
+    chunk_load(0)[0].wait()
+    for copy in chunk_load(3):
+        copy.start()
+    both[0] = dot(tokens[0:CHUNK], sides[...])
+    up_load.wait()
+
+    @pl.loop(1, chunks)
+    def _(chunk):
+        chunk_load(chunk - 1)[1].wait()
+        chunk_load(chunk)[0].wait()
+        spread(chunk - 1)
+        both[chunk % 2] = dot(tokens[span(chunk * CHUNK, CHUNK, CHUNK)], sides[...])
+
+    frozen_load.start()
+    chunk_load(chunks - 1)[1].wait()
+    spread(chunks - 1)
+    pl.semaphore_wait(barrier, len(greeted))
+    statistics.start(0)
+
     def down_block(start, size):
         here = pl.ds(start, size)
         part[here] = dot(grads_t[...], tokens[:, here]).T
@@ -389,8 +408,6 @@
     down_block(0, 896)
     down_block(896, 896)
     exchange.start(0, pieces[0])
-    statistics.finish(0)
-    statistics.start(1)
     down_block(1792, 896)
     down_block(2688, 896)
     exchange.start(0, pieces[1])
@@ -399,8 +416,8 @@
     for block in range(outputs // LANES):
         part[up_base + block * LANES : up_base + (block + 1) * LANES] = found[:, block * LANES : (block + 1) * LANES]
     exchange.start(0, pieces[2])
-    statistics.finish(1)
-    statistics.start(2)
+    statistics.finish(0)
+    statistics.start(1)
     exchange.step(0, pieces[0])
     group = lax.broadcasted_iota(jnp.int32, (2 * ranks, ranks), 0) % ranks // rank
     member = lax.broadcasted_iota(jnp.int32, (2 * ranks, ranks), 1) // rank
@@ -415,7 +432,12 @@
         task = 2.0 * dot(jnp.concatenate([upper, lower], axis=1), blocks)
         plain[here] += share * (task - lane_sum(share * task) * scale)
 
+    task_part(0)
+    task_part(1)
     exchange.step(0, pieces[1])
+    task_part(2)
+    task_part(3)
+    exchange.step(0, pieces[2])
     lane = lax.broadcasted_iota(jnp.int32, (CHUNK, LANES), 1)
     pick_from = lax.broadcasted_iota(jnp.int32, (ranks, ranks), 0)
     pick_to = lax.broadcasted_iota(jnp.int32, (ranks, ranks), 1)
@@ -423,7 +445,7 @@
     pick = jnp.where(pick_to < 2 * experts, pick, 0.0).astype(BF16)
 
     def slope_part(chunk):
-        load_all, live_all = tiles[3, 0:1], tiles[3, 2:3]
+        load_all, live_all = tiles[2, 0:1], tiles[2, 2:3]
         push = (2.0 * experts * 100.0) / live_all
         here = span(chunk * CHUNK, CHUNK, CHUNK)
         share = prob[here]
@@ -445,22 +467,29 @@
         for piece in pieces[:3]:
             exchange.step(phase, piece)
 
+    def at(block, place):
+        return pl.when(block == place)
+
     frozen_load.wait()
-    exchange.step(0, pieces[2])
-
-    @pl.loop(0, 2)
+
+    @pl.loop(0, 3)
     def _(block):
-        task_part(2 * block)
-        task_part(2 * block + 1)
         base_block(block)
 
-    statistics.finish(2)
-
-    @pl.loop(2, 4)
+    statistics.finish(1)
+
+    @pl.loop(3, 5)
     def _(block):
-        slope_part(2 * block - 4)
-        slope_part(2 * block - 3)
+        @at(block, 4)
+        def _():
+            exchange.step(1, pieces[0])
+
+        slope_part(2 * block - 6)
+        slope_part(2 * block - 5)
         base_block(block)
+
+    exchange.step(1, pieces[1])
+    exchange.step(1, pieces[2])
 
     @pl.loop(0, width // 1024)
     def _(block):
@@ -472,47 +501,52 @@
 
     gates.start(0)
 
-    @pl.loop(4, 8)
+    @pl.loop(5, 8)
     def _(block):
-        @pl.when(block == 4)
+        @at(block, 6)
         def _():
-            exchange.step(1, pieces[0])
-
-        @pl.when(block == 5)
+            exchange.step(2, pieces[0])
+
+        @at(block, 7)
         def _():
-            exchange.step(1, pieces[1])
-            exchange.step(1, pieces[2])
-
-        @pl.when(block == 7)
-        def _():
-            step_all(2)
-            gates.step(0)
+            exchange.step(2, pieces[1])
+            exchange.step(2, pieces[2])
 
         base_block(block)
 
     @pl.loop(0, input_ref.shape[1] // 512)
     def _(block):
-        @pl.when(block == 1)
+        @at(block, 0)
         def _():
-            step_all(3)
-
-        @pl.when(block == 2)
+            gates.step(0)
+
+        @at(block, 1)
+        def _():
+            exchange.step(3, pieces[0])
+
+        @at(block, 2)
         def _():
             gates.step(1)
-
-        @pl.when(block == 3)
+            exchange.step(3, pieces[1])
+            exchange.step(3, pieces[2])
+
+        @at(block, 3)
         def _():
-            step_all(4)
-
-        @pl.when(block == 5)
+            exchange.step(4, pieces[0])
+
+        @at(block, 4)
         def _():
-            step_all(5)
+            gates.step(2)
+            exchange.step(4, pieces[1])
+            exchange.step(4, pieces[2])
 
         here = span(block * 512, 512, 512)
         found = right_dot(masked[...], frozen[here]) + right_dot(grads[...], sides[here])
         input_ref[:, here] = found.astype(BF16)
 
-    gates.finish(2)
+    for piece in pieces:
+        exchange.step(5, piece)
+    gates.finish(3)
     for piece in pieces:
         exchange.finish(6, piece)
 
@@ -566,7 +600,7 @@
         copy = pltpu.make_async_copy(rest.at[block], input_hbm.at[:, here], sems.at[8 + block])
         copy.start()
         copies.append(copy)
-    mean = tiles[3] / tiles[3, 2:3]
+    mean = tiles[2] / tiles[2, 2:3]
     lane = lax.broadcasted_iota(jnp.int32, (1, LANES), 1)
     for expert in range(experts):
         load_ref[expert] = jnp.sum(jnp.where(lane == expert * rank, mean[0:1], 0.0))
@@ -590,7 +624,7 @@
             pltpu.VMEM((rows, outputs), BF16),
             pltpu.VMEM((rows, width - 1024), BF16),
             pltpu.VMEM((every, LANES), F32),
-            pltpu.VMEM((4, 8, LANES), F32),
+            pltpu.VMEM((3, 8, LANES), F32),
             pltpu.VMEM((width, outputs), BF16),
             pltpu.VMEM((width, 2 * ranks), BF16),
             pltpu.VMEM((rows, outputs), BF16),
@@ -618,16 +652,16 @@
             pltpu.VMEM((3, every // 32, LANES), F32),
             pltpu.VMEM((4, every // 32, LANES), F32),
             pltpu.VMEM((8, 8, LANES), F32),
-            pltpu.VMEM((2, SIDE, 8, LANES), F32),
+            pltpu.VMEM((16, 8, LANES), F32),
             pltpu.VMEM((7, width * experts // LANES // 8, LANES), F32),
-            pltpu.VMEM((16, width * experts // LANES // 8, LANES), F32),
-            pltpu.SemaphoreType.DMA((6,)),
-            pltpu.SemaphoreType.DMA((rows // CHUNK,)),
+            pltpu.VMEM((2, SIDE, width * experts // LANES // 8, LANES), F32),
+            pltpu.SemaphoreType.DMA((5,)),
+            pltpu.SemaphoreType.DMA((rows // CHUNK, 2)),
             pltpu.SemaphoreType.DMA((4,)),
-            pltpu.SemaphoreType.DMA((7, 3)),
+            pltpu.SemaphoreType.DMA((8, 3)),
             pltpu.SemaphoreType.DMA((1,)),
-            pltpu.SemaphoreType.DMA((3,)),
-            pltpu.SemaphoreType.DMA((3,)),
+            pltpu.SemaphoreType.DMA((2,)),
+            pltpu.SemaphoreType.DMA((4,)),
         ],
         compiler_params=pltpu.CompilerParams(
             collective_id=0, has_side_effects=True, vmem_limit_bytes=34 * 1024 * 1024

time: 54.8 us -> 52.1 us (0.951)
  Pallas kernels: 54.1 us -> 51.3 us
    pallas_call x1, Pallas kernels: 48.4 us -> 45.6 us  [on_device(): pl.pallas_call(functools.partial(kernel, (rows, width, outputs, ranks, ex...]
where the time goes in v5:
time: 52.1 us; the launch traced here: 52 us
  Pallas kernels  51.3 us (98%)
  between operations  0.64 us (1%)
    pallas_call x1, Pallas kernels, on_device(): pl.pallas_call(functools.partial(kernel, (rows, width, outputs, ranks, ex...  45.6 us
    pallas_call x1, Pallas kernels, on_device(): pl.pallas_call(functools.partial(finish_kernel, (width, outputs, ranks, e...  5.69 us

profile of v5, /device:TPU:1, one launch (start us, length us, event | category | flops | bytes accessed | tf_op | source)
XLA Modules:
  0.0 52.0 jit_solution(8026739157882244192)
XLA Ops:
  0.6 45.6 %step.1 = (bf16[1024,1024]{1,0:T(8,128)(2,1)S(1)}, bf16[1024,3072]{1,0:T(8,128)(2,1)S(1)}, f32[5376,128]{1,0:T(8,128)S(1)}, f32[3,8,128]{2,1,0:T(8,128)S(1)}, bf...) custom-call(s32[8,128]{1,0:T(8,128)} %bitcast.5, ...), custom_call_target="tpu_custom_call" | custom-call | tf_op jit(solution)/shard_map/step/pallas_call | solution.py:621
  46.3 5.7 %finish.1 = (bf16[1024,1024]{1,0:T(8,128)(2,1)}, bf16[1024,4096]{1,0:T(8,128)(2,1)}, f32[4096,128]{1,0:T(8,128)}, f32[128,1024]{1,0:T(8,128)}, f32[8,4096]{1,0:T(8,128)}, /*index=5*/f32[8]{0:T(128)}, f32[1]{0:T(128)}) custom-call(bf16[1024,1024]{1,0:T(8,128)(2,1)S(1)} %get-tuple-element.22.projected, bf16[1024,3072]{1,0:T(8,128)(2,1)S(1)} %get-tuple-element.23.inputs, ...), custom_call_target="tpu_custom_call" | custom-call | tf_op jit(solution)/shard_map/finish/pallas_call | solution.py:671

commit v6 on v5

--- a/solution.py
+++ b/solution.py
@@ -304,11 +304,6 @@
     ids_load = pltpu.make_async_copy(ids_hbm, ids, load_sem.at[1])
     gate_load.start()
     ids_load.start()
-    barrier = pltpu.get_barrier_semaphore()
-    greeted = peers()
-    for peer in greeted:
-        pl.semaphore_signal(barrier, inc=1, device_id=peer, device_id_type=MESH)
-
     def load(source, target, slot):
         return pltpu.make_async_copy(source, target, load_sem.at[slot])
 
@@ -326,6 +321,10 @@
     chunk_load(0)[0].start()
     up_load.start()
     chunk_load(0)[1].start()
+    barrier = pltpu.get_barrier_semaphore()
+    greeted = peers()
+    for peer in greeted:
+        pl.semaphore_signal(barrier, inc=1, device_id=peer, device_id_type=MESH)
 
     gate_load.wait()
     for copy in chunk_load(1):
@@ -402,8 +401,10 @@
     statistics.start(0)
 
     def down_block(start, size):
-        here = pl.ds(start, size)
-        part[here] = dot(grads_t[...], tokens[:, here]).T
+        found = dot(grads_t[...], tokens[:, pl.ds(start, size)])
+        for block in range(size // LANES):
+            here = start + block * LANES
+            part[here : here + LANES] = found[:, block * LANES : (block + 1) * LANES]
 
     down_block(0, 896)
     down_block(896, 896)
@@ -526,9 +527,9 @@
 
         @at(block, 2)
         def _():
-            gates.step(1)
             exchange.step(3, pieces[1])
             exchange.step(3, pieces[2])
+            gates.step(1)
 
         @at(block, 3)
         def _():
@@ -536,16 +537,23 @@
 
         @at(block, 4)
         def _():
-            gates.step(2)
             exchange.step(4, pieces[1])
             exchange.step(4, pieces[2])
+
+        @at(block, 5)
+        def _():
+            gates.step(2)
+
+        @at(block, 6)
+        def _():
+            exchange.step(5, pieces[0])
 
         here = span(block * 512, 512, 512)
         found = right_dot(masked[...], frozen[here]) + right_dot(grads[...], sides[here])
         input_ref[:, here] = found.astype(BF16)
 
-    for piece in pieces:
-        exchange.step(5, piece)
+    exchange.step(5, pieces[1])
+    exchange.step(5, pieces[2])
     gates.finish(3)
     for piece in pieces:
         exchange.finish(6, piece)
@@ -554,19 +562,25 @@
 def finish_kernel(
     sizes,
     projected, inputs, total, tiles, frozen, sides, masked, grads,
-    projected_hbm, input_hbm, down_hbm, up_hbm, gate_hbm, load_ref, entropy_ref,
-    scaled, up, gate, rest, sems,
+    projected_hbm, input_hbm, down_hbm, up_hbm, gate_hbm, load_hbm, entropy_hbm,
+    scaled, up, gate, rest, load, entropy, sems,
 ):
     width, outputs, ranks, experts = sizes
     rank = ranks // experts
     every = total.shape[0]
-    quarter = width // 4
-    copies = [
-        pltpu.make_async_copy(inputs, input_hbm.at[:, pl.ds(0, inputs.shape[1])], sems.at[0]),
-        pltpu.make_async_copy(projected, projected_hbm, sems.at[1]),
-    ]
-    for copy in copies:
+    done = inputs.shape[1]
+    copies = []
+
+    def send(source, target):
+        copy = pltpu.make_async_copy(source, target, sems.at[len(copies)])
         copy.start()
+        copies.append(copy)
+
+    tall = inputs.shape[0] // 4
+    for block in range(4):
+        here = pl.ds(block * tall, tall)
+        send(inputs.at[here], input_hbm.at[here, pl.ds(0, done)])
+    send(projected, projected_hbm)
 
     def add_squares(block, found):
         value = total[span(block * 192, 192)]
@@ -574,37 +588,31 @@
 
     squares = lax.fori_loop(0, every // 192, add_squares, jnp.zeros((32, LANES), F32))
     norm = jnp.sqrt(jnp.sum(jnp.sum(squares, axis=1, keepdims=True), axis=0, keepdims=True))
+    mean = tiles[2] / tiles[2, 2:3]
+    lane = lax.broadcasted_iota(jnp.int32, (1, LANES), 1)
+    for expert in range(experts):
+        load[expert] = jnp.sum(jnp.where(lane == expert * rank, mean[0:1], 0.0))
+    entropy[0] = jnp.sum(jnp.where(lane == 0, mean[1:2], 0.0))
+    send(load, load_hbm)
+    send(entropy, entropy_hbm)
+
+    here = pl.ds(done, 512)
+    found = right_dot(masked[...], frozen[here]) + right_dot(grads[...], sides[here])
+    rest[...] = found.astype(BF16)
     factor = jnp.minimum(1.0, math.sqrt(every * LANES) / norm)
-    for block in range(4):
-        here = pl.ds(block * quarter, quarter)
-        scaled[here] = total[here] * factor
-        copy = pltpu.make_async_copy(scaled.at[here], down_hbm.at[here], sems.at[2 + block])
-        copy.start()
-        copies.append(copy)
+    for block in range(width // LANES):
+        here = pl.ds(block * LANES, LANES)
+        scaled[here] = (total[here] * factor).T
     for block in range(outputs // LANES):
         here = width + block * LANES
         up[:, block * LANES : (block + 1) * LANES] = total[here : here + LANES] * factor
-    copy = pltpu.make_async_copy(up, up_hbm, sems.at[6])
-    copy.start()
-    copies.append(copy)
     for block in range(width // LANES):
         here = width + outputs + block * experts
         gate[:, block * LANES : (block + 1) * LANES] = total[here : here + experts] * factor
-    copy = pltpu.make_async_copy(gate, gate_hbm, sems.at[7])
-    copy.start()
-    copies.append(copy)
-    for block in range(2):
-        here = pl.ds(inputs.shape[1] + block * 512, 512)
-        found = right_dot(masked[...], frozen[here]) + right_dot(grads[...], sides[here])
-        rest[block] = found.astype(BF16)
-        copy = pltpu.make_async_copy(rest.at[block], input_hbm.at[:, here], sems.at[8 + block])
-        copy.start()
-        copies.append(copy)
-    mean = tiles[2] / tiles[2, 2:3]
-    lane = lax.broadcasted_iota(jnp.int32, (1, LANES), 1)
-    for expert in range(experts):
-        load_ref[expert] = jnp.sum(jnp.where(lane == expert * rank, mean[0:1], 0.0))
-    entropy_ref[0] = jnp.sum(jnp.where(lane == 0, mean[1:2], 0.0))
+    send(scaled, down_hbm)
+    send(up, up_hbm)
+    send(gate, gate_hbm)
+    send(rest, input_hbm.at[:, pl.ds(done, 512)])
     for copy in copies:
         copy.wait()
 
@@ -617,12 +625,11 @@
     anywhere = pl.BlockSpec(memory_space=pl.ANY)
     hbm = pl.BlockSpec(memory_space=pltpu.HBM)
     vmem = pl.BlockSpec(memory_space=pltpu.VMEM)
-    smem = pl.BlockSpec(memory_space=pltpu.SMEM)
     held = pl.pallas_call(
         functools.partial(kernel, (rows, width, outputs, ranks, experts)),
         out_shape=(
             pltpu.VMEM((rows, outputs), BF16),
-            pltpu.VMEM((rows, width - 1024), BF16),
+            pltpu.VMEM((rows, width - 512), BF16),
             pltpu.VMEM((every, LANES), F32),
             pltpu.VMEM((3, 8, LANES), F32),
             pltpu.VMEM((width, outputs), BF16),
@@ -664,7 +671,7 @@
             pltpu.SemaphoreType.DMA((4,)),
         ],
         compiler_params=pltpu.CompilerParams(
-            collective_id=0, has_side_effects=True, vmem_limit_bytes=34 * 1024 * 1024
+            collective_id=0, has_side_effects=True, vmem_limit_bytes=36 * 1024 * 1024
         ),
         name="step",
     )(token_ids.reshape(rows // LANES, LANES), tokens, frozen_weight, adapter_down, adapter_up, gate_weight.T, upstream)
@@ -680,15 +687,17 @@
             jax.ShapeDtypeStruct((1,), F32),
         ),
         in_specs=[vmem] * 8,
-        out_specs=(anywhere,) * 5 + (smem,) * 2,
+        out_specs=(anywhere,) * 7,
         scratch_shapes=[
             pltpu.VMEM((width, ranks), F32),
             pltpu.VMEM((ranks, outputs), F32),
             pltpu.VMEM((experts, width), F32),
-            pltpu.VMEM((2, rows, 512), BF16),
-            pltpu.SemaphoreType.DMA((10,)),
+            pltpu.VMEM((rows, 512), BF16),
+            pltpu.SMEM((experts,), F32),
+            pltpu.SMEM((1,), F32),
+            pltpu.SemaphoreType.DMA((11,)),
         ],
-        compiler_params=pltpu.CompilerParams(vmem_limit_bytes=16 * 1024 * 1024),
+        compiler_params=pltpu.CompilerParams(vmem_limit_bytes=12 * 1024 * 1024),
         name="finish",
     )(*held)
     return projected, input_grad, down, up, gate.T, load, entropy.reshape(())

time: 52.1 us -> 51.6 us (level)
    pallas_call x1, Pallas kernels: 5.69 us -> 4.89 us  [on_device(): pl.pallas_call(functools.partial(finish_kernel, (width, outputs, ranks, e...]
where the time goes in v6:
time: 51.6 us; the launch traced here: 51.5 us
  Pallas kernels  50.9 us (99%)
  between operations  0.64 us (1%)
    pallas_call x1, Pallas kernels, on_device(): pl.pallas_call(functools.partial(kernel, (rows, width, outputs, ranks, ex...  46 us
    pallas_call x1, Pallas kernels, on_device(): pl.pallas_call(functools.partial(finish_kernel, (width, outputs, ranks, e...  4.89 us

profile of v6, /device:TPU:1, one launch (start us, length us, event | category | flops | bytes accessed | tf_op | source)
XLA Modules:
  0.0 51.5 jit_solution(8691450900646353857)
XLA Ops:
  0.6 46.0 %step.1 = (bf16[1024,1024]{1,0:T(8,128)(2,1)S(1)}, bf16[1024,3584]{1,0:T(8,128)(2,1)S(1)}, f32[5376,128]{1,0:T(8,128)S(1)}, f32[3,8,128]{2,1,0:T(8,128)S(1)}, bf...) custom-call(s32[8,128]{1,0:T(8,128)} %bitcast.5, ...), custom_call_target="tpu_custom_call" | custom-call | tf_op jit(solution)/shard_map/step/pallas_call | solution.py:628
  46.6 4.9 %finish.1 = (bf16[1024,1024]{1,0:T(8,128)(2,1)}, bf16[1024,4096]{1,0:T(8,128)(2,1)}, f32[4096,128]{1,0:T(8,128)}, f32[128,1024]{1,0:T(8,128)}, f32[8,4096]{1,0:T(8,128)}, /*index=5*/f32[8]{0:T(128)}, f32[1]{0:T(128)}) custom-call(bf16[1024,1024]{1,0:T(8,128)(2,1)S(1)} %get-tuple-element.22.projected, bf16[1024,3584]{1,0:T(8,128)(2,1)S(1)} %get-tuple-element.23.inputs, ...), custom_call_target="tpu_custom_call" | custom-call | tf_op jit(solution)/shard_map/finish/pallas_call | solution.py:678

commit v7 on v6

--- a/solution.py
+++ b/solution.py
@@ -283,8 +283,8 @@
 def kernel(
     sizes,
     ids_hbm, tokens_hbm, frozen_hbm, down_hbm, up_hbm, gate_hbm, upstream_hbm,
-    projected_ref, input_ref, total, tiles, frozen, sides, masked, grads,
-    ids, tokens, up, gate,
+    projected_ref, input_ref, total, tiles,
+    ids, tokens, frozen, sides, masked, grads, up, gate,
     both, low, prob, plain, turned, weighted, grads_t, weighted_t, gate_t,
     part, halves, firsts, seconds, thirds, wide, plane, inward, rings,
     load_sem, token_sem, send, recv, stat_send, stat_recv, gate_recv,
@@ -406,20 +406,15 @@
             here = start + block * LANES
             part[here : here + LANES] = found[:, block * LANES : (block + 1) * LANES]
 
-    down_block(0, 896)
-    down_block(896, 896)
+    down_block(0, 1792)
     exchange.start(0, pieces[0])
-    down_block(1792, 896)
-    down_block(2688, 896)
+    down_block(1792, 1792)
     exchange.start(0, pieces[1])
     down_block(3584, 512)
     found = dot(weighted_t[...], masked[...])
     for block in range(outputs // LANES):
         part[up_base + block * LANES : up_base + (block + 1) * LANES] = found[:, block * LANES : (block + 1) * LANES]
     exchange.start(0, pieces[2])
-    statistics.finish(0)
-    statistics.start(1)
-    exchange.step(0, pieces[0])
     group = lax.broadcasted_iota(jnp.int32, (2 * ranks, ranks), 0) % ranks // rank
     member = lax.broadcasted_iota(jnp.int32, (2 * ranks, ranks), 1) // rank
     blocks = (group == member).astype(F32).astype(BF16)
@@ -435,8 +430,11 @@
 
     task_part(0)
     task_part(1)
+    statistics.finish(0)
+    statistics.start(1)
+    exchange.step(0, pieces[0])
+    task_part(2)
     exchange.step(0, pieces[1])
-    task_part(2)
     task_part(3)
     exchange.step(0, pieces[2])
     lane = lax.broadcasted_iota(jnp.int32, (CHUNK, LANES), 1)
@@ -492,12 +490,12 @@
     exchange.step(1, pieces[1])
     exchange.step(1, pieces[2])
 
-    @pl.loop(0, width // 1024)
+    @pl.loop(0, width // 2048)
     def _(block):
-        found = dot(gate_t[...], tokens[:, span(block * 1024, 1024, 1024)])
+        found = dot(gate_t[...], tokens[:, span(block * 2048, 2048, 2048)])
         found = found[:experts] + found[experts:]
-        for piece in range(8):
-            here = span(gate_base + (block * 8 + piece) * experts, experts)
+        for piece in range(16):
+            here = span(gate_base + (block * 16 + piece) * experts, experts)
             part[here] = found[:, piece * LANES : (piece + 1) * LANES]
 
     gates.start(0)
@@ -515,7 +513,12 @@
 
         base_block(block)
 
-    @pl.loop(0, input_ref.shape[1] // 512)
+    def input_block(block):
+        here = span(block * 512, 512, 512)
+        found = right_dot(masked[...], frozen[here]) + right_dot(grads[...], sides[here])
+        input_ref[:, here] = found.astype(BF16)
+
+    @pl.loop(0, input_ref.shape[1] // 512 - 1)
     def _(block):
         @at(block, 0)
         def _():
@@ -548,12 +551,11 @@
         def _():
             exchange.step(5, pieces[0])
 
-        here = span(block * 512, 512, 512)
-        found = right_dot(masked[...], frozen[here]) + right_dot(grads[...], sides[here])
-        input_ref[:, here] = found.astype(BF16)
+        input_block(block)
 
     exchange.step(5, pieces[1])
     exchange.step(5, pieces[2])
+    input_block(input_ref.shape[1] // 512 - 1)
     gates.finish(3)
     for piece in pieces:
         exchange.finish(6, piece)
@@ -561,14 +563,13 @@
 
 def finish_kernel(
     sizes,
-    projected, inputs, total, tiles, frozen, sides, masked, grads,
+    projected, inputs, total, tiles,
     projected_hbm, input_hbm, down_hbm, up_hbm, gate_hbm, load_hbm, entropy_hbm,
-    scaled, up, gate, rest, load, entropy, sems,
+    scaled, up, gate, load, entropy, sems,
 ):
     width, outputs, ranks, experts = sizes
     rank = ranks // experts
     every = total.shape[0]
-    done = inputs.shape[1]
     copies = []
 
     def send(source, target):
@@ -579,7 +580,7 @@
     tall = inputs.shape[0] // 4
     for block in range(4):
         here = pl.ds(block * tall, tall)
-        send(inputs.at[here], input_hbm.at[here, pl.ds(0, done)])
+        send(inputs.at[here], input_hbm.at[here])
     send(projected, projected_hbm)
 
     def add_squares(block, found):
@@ -596,9 +597,6 @@
     send(load, load_hbm)
     send(entropy, entropy_hbm)
 
-    here = pl.ds(done, 512)
-    found = right_dot(masked[...], frozen[here]) + right_dot(grads[...], sides[here])
-    rest[...] = found.astype(BF16)
     factor = jnp.minimum(1.0, math.sqrt(every * LANES) / norm)
     for block in range(width // LANES):
         here = pl.ds(block * LANES, LANES)
@@ -612,7 +610,6 @@
     send(scaled, down_hbm)
     send(up, up_hbm)
     send(gate, gate_hbm)
-    send(rest, input_hbm.at[:, pl.ds(done, 512)])
     for copy in copies:
         copy.wait()
 
@@ -629,19 +626,19 @@
         functools.partial(kernel, (rows, width, outputs, ranks, experts)),
         out_shape=(
             pltpu.VMEM((rows, outputs), BF16),
-            pltpu.VMEM((rows, width - 512), BF16),
+            pltpu.VMEM((rows, width), BF16),
             pltpu.VMEM((every, LANES), F32),
             pltpu.VMEM((3, 8, LANES), F32),
+        ),
+        in_specs=[hbm] * 7,
+        out_specs=(vmem,) * 4,
+        scratch_shapes=[
+            pltpu.VMEM((rows // LANES, LANES), jnp.int32),
+            pltpu.VMEM((rows, width), BF16),
             pltpu.VMEM((width, outputs), BF16),
             pltpu.VMEM((width, 2 * ranks), BF16),
             pltpu.VMEM((rows, outputs), BF16),
             pltpu.VMEM((rows, 2 * ranks), BF16),
-        ),
-        in_specs=[hbm] * 7,
-        out_specs=(vmem,) * 8,
-        scratch_shapes=[
-            pltpu.VMEM((rows // LANES, LANES), jnp.int32),
-            pltpu.VMEM((rows, width), BF16),
             pltpu.VMEM((ranks, outputs), BF16),
             pltpu.VMEM((experts, width), BF16),
             pltpu.VMEM((2, CHUNK, 2 * ranks), F32),
@@ -671,7 +668,7 @@
             pltpu.SemaphoreType.DMA((4,)),
         ],
         compiler_params=pltpu.CompilerParams(
-            collective_id=0, has_side_effects=True, vmem_limit_bytes=36 * 1024 * 1024
+            collective_id=0, has_side_effects=True, vmem_limit_bytes=46 * 1024 * 1024
         ),
         name="step",
     )(token_ids.reshape(rows // LANES, LANES), tokens, frozen_weight, adapter_down, adapter_up, gate_weight.T, upstream)
@@ -686,16 +683,15 @@
             jax.ShapeDtypeStruct((experts,), F32),
             jax.ShapeDtypeStruct((1,), F32),
         ),
-        in_specs=[vmem] * 8,
+        in_specs=[vmem] * 4,
         out_specs=(anywhere,) * 7,
         scratch_shapes=[
             pltpu.VMEM((width, ranks), F32),
             pltpu.VMEM((ranks, outputs), F32),
             pltpu.VMEM((experts, width), F32),
-            pltpu.VMEM((rows, 512), BF16),
             pltpu.SMEM((experts,), F32),
             pltpu.SMEM((1,), F32),
-            pltpu.SemaphoreType.DMA((11,)),
+            pltpu.SemaphoreType.DMA((10,)),
         ],
         compiler_params=pltpu.CompilerParams(vmem_limit_bytes=12 * 1024 * 1024),
         name="finish",

time: 51.6 us -> 51.2 us (level)
  no operation moved by 1% of the time
where the time goes in v7:
time: 51.2 us; the launch traced here: 51 us
  Pallas kernels  50.4 us (98%)
  between operations  0.64 us (1%)
    pallas_call x1, Pallas kernels, on_device(): pl.pallas_call(functools.partial(kernel, (rows, width, outputs, ranks, ex...  45.6 us
    pallas_call x1, Pallas kernels, on_device(): pl.pallas_call(functools.partial(finish_kernel, (width, outputs, ranks, e...  4.81 us

profile of v7, /device:TPU:1, one launch (start us, length us, event | category | flops | bytes accessed | tf_op | source)
XLA Modules:
  0.0 51.0 jit_solution(17252285773247557850)
XLA Ops:
  0.6 45.6 %step.1 = (bf16[1024,1024]{1,0:T(8,128)(2,1)S(1)}, bf16[1024,4096]{1,0:T(8,128)(2,1)S(1)}, f32[5376,128]{1,0:T(8,128)S(1)}, f32[3,8,128]{2,1,0:T(8,128)S(1)}) custom-call(s32[8,128]{1,0:T(8,128)} %bitcast.5, bf16[1024,4096]{1,0:T(8,128)(2,1)} %tokens_hbm.1, bf16[4096,1024]{1,0:T(8,128)(2,1)} %frozen_hbm.1, bf16[4096,128]{1,0:T(8,128)(2,1)} %down_hbm.1, ...), custom_call_target="tpu_custom_call" | custom-call | tf_op jit(solution)/shard_map/step/pallas_call | solution.py:625
  46.2 4.8 %finish.1 = (bf16[1024,1024]{1,0:T(8,128)(2,1)}, bf16[1024,4096]{1,0:T(8,128)(2,1)}, f32[4096,128]{1,0:T(8,128)}, f32[128,1024]{1,0:T(8,128)}, f32[8,4096]{1,0:T(8,128)}, /*index=5*/f32[8]{0:T(128)}, f32[1]{0:T(128)}) custom-call(bf16[1024,1024]{1,0:T(8,128)(2,1)S(1)} %get-tuple-element.18.projected, bf16[1024,4096]{1,0:T(8,128)(2,1)S(1)} %get-tuple-element.19.inputs, ...), custom_call_target="tpu_custom_call" | custom-call | tf_op jit(solution)/shard_map/finish/pallas_call | solution.py:675

commit v8 on v7

--- a/solution.py
+++ b/solution.py
@@ -471,24 +471,21 @@
 
     frozen_load.wait()
 
-    @pl.loop(0, 3)
-    def _(block):
-        base_block(block)
+    first = pl.ds(0, 256)
+    found = dot(tokens[...], frozen[:, first]) + dot(weighted[...], up[:, first])
+    projected_ref[:, first] = found.astype(BF16)
+    base_block(2)
 
     statistics.finish(1)
 
     @pl.loop(3, 5)
     def _(block):
-        @at(block, 4)
-        def _():
-            exchange.step(1, pieces[0])
-
         slope_part(2 * block - 6)
         slope_part(2 * block - 5)
         base_block(block)
 
-    exchange.step(1, pieces[1])
-    exchange.step(1, pieces[2])
+    for piece in pieces:
+        exchange.step(1, piece)
 
     @pl.loop(0, width // 2048)
     def _(block):

time: 51.2 us -> 50.5 us (0.986)
  Pallas kernels: 50.4 us -> 49.8 us
    pallas_call x1, Pallas kernels: 45.6 us -> 45 us  [on_device(): pl.pallas_call(functools.partial(kernel, (rows, width, outputs, ranks, ex...]
where the time goes in v8:
time: 50.5 us; the launch traced here: 50.4 us
  Pallas kernels  49.8 us (99%)
  between operations  0.64 us (1%)
    pallas_call x1, Pallas kernels, on_device(): pl.pallas_call(functools.partial(kernel, (rows, width, outputs, ranks, ex...  45 us
    pallas_call x1, Pallas kernels, on_device(): pl.pallas_call(functools.partial(finish_kernel, (width, outputs, ranks, e...  4.81 us

profile of v8, /device:TPU:1, one launch (start us, length us, event | category | flops | bytes accessed | tf_op | source)
XLA Modules:
  0.0 50.4 jit_solution(2216559995769170430)
XLA Ops:
  0.6 45.0 %step.1 = (bf16[1024,1024]{1,0:T(8,128)(2,1)S(1)}, bf16[1024,4096]{1,0:T(8,128)(2,1)S(1)}, f32[5376,128]{1,0:T(8,128)S(1)}, f32[3,8,128]{2,1,0:T(8,128)S(1)}) custom-call(s32[8,128]{1,0:T(8,128)} %bitcast.5, bf16[1024,4096]{1,0:T(8,128)(2,1)} %tokens_hbm.1, bf16[4096,1024]{1,0:T(8,128)(2,1)} %frozen_hbm.1, bf16[4096,128]{1,0:T(8,128)(2,1)} %down_hbm.1, ...), custom_call_target="tpu_custom_call" | custom-call | tf_op jit(solution)/shard_map/step/pallas_call | solution.py:622
  45.6 4.8 %finish.1 = (bf16[1024,1024]{1,0:T(8,128)(2,1)}, bf16[1024,4096]{1,0:T(8,128)(2,1)}, f32[4096,128]{1,0:T(8,128)}, f32[128,1024]{1,0:T(8,128)}, f32[8,4096]{1,0:T(8,128)}, /*index=5*/f32[8]{0:T(128)}, f32[1]{0:T(128)}) custom-call(bf16[1024,1024]{1,0:T(8,128)(2,1)S(1)} %get-tuple-element.18.projected, bf16[1024,4096]{1,0:T(8,128)(2,1)S(1)} %get-tuple-element.19.inputs, ...), custom_call_target="tpu_custom_call" | custom-call | tf_op jit(solution)/shard_map/finish/pallas_call | solution.py:672
